TPU v7x, 128 devices: a whole 4x4x4 slice. The times are simulated.
128 devices in a mesh: tm: 32 (over x, y, core), batch: 4 (over z).
Axes of the slice: x: 4, y: 4, z: 4, core: 2. Of those that a mesh axis runs over, the one named last changes fastest.
Arguments:
- hidden_states: bfloat16 [4, 4096, 5120], P('batch', 'tm'), may hold values from -6 to 6
- gen_weight: bfloat16 [64, 5120], replicated, may hold values from -0.078125 to 0.078125
- noise_field: bfloat16 [4, 64, 4096], P('batch', None, 'tm'), may hold values from -6 to 6
- timesteps: int32 [4], P('batch'), may hold values from 200 to 999
- embed_real: bfloat16 [128, 5120], replicated, may hold values from -0.5 to 0.5
- time_real: bfloat16 [256, 3, 5120], P('tm'), may hold values from -0.375 to 0.375
- query_real: bfloat16 [5120, 4096], P(None, 'tm'), may hold values from -3 to 3
- key_real: bfloat16 [5120, 4096], P(None, 'tm'), may hold values from -3 to 3
- value_real: bfloat16 [5120, 4096], P(None, 'tm'), may hold values from -0.078125 to 0.078125
- out_real: bfloat16 [4096, 5120], P('tm'), may hold values from -0.09375 to 0.09375
- gain_real: float32 [2, 4096], P(None, 'tm'), may hold values from 0.25 to 3
- proj_real: bfloat16 [64, 5120], replicated, may hold values from -0.078125 to 0.078125
- embed_fake: bfloat16 [128, 5120], replicated, may hold values from -0.5 to 0.5
- time_fake: bfloat16 [256, 3, 5120], P('tm'), may hold values from -0.375 to 0.375
- query_fake: bfloat16 [5120, 4096], P(None, 'tm'), may hold values from -3 to 3
- key_fake: bfloat16 [5120, 4096], P(None, 'tm'), may hold values from -3 to 3
- value_fake: bfloat16 [5120, 4096], P(None, 'tm'), may hold values from -0.078125 to 0.078125
- out_fake: bfloat16 [4096, 5120], P('tm'), may hold values from -0.09375 to 0.09375
- gain_fake: float32 [2, 4096], P(None, 'tm'), may hold values from 0.25 to 3
- proj_fake: bfloat16 [64, 5120], replicated, may hold values from -0.078125 to 0.078125
Outputs:
- dmd_gradient: float32 [4, 64, 4096], P('batch', None, 'tm')
- weight_grad: float32 [64, 5120], replicated
All inputs are finite; a program needn't handle non-finite values.
Results may differ from a plain program's by a relative error of at most 0.019.
Values may be sent and summed in bfloat16 or wider, within the bound.
A program may use at most 128 MiB of HBM per device.

v0:
```python
import math

import jax
import jax.numpy as jnp
from jax import lax
from jax.sharding import PartitionSpec as P

HD = 128
FREQ = 256
FTOK = 128


norm_floor = 0.05
gap_floor = 0.25
highest = lax.Precision.HIGHEST


def copy_for_each(shard, axis):
    copies = jnp.broadcast_to(shard, (lax.axis_size(axis), *shard.shape))
    return lax.all_to_all(copies, axis, split_axis=0, concat_axis=0, tiled=True)


def over_copies(shard, axis):
    return copy_for_each(shard, axis).sum(axis=0)


def together(arrays, axis):
    ends = [0]
    for a in arrays:
        ends.append(ends[-1] + a.size)
    so_far = over_copies(jnp.concatenate([a.ravel() for a in arrays]), axis)
    return tuple((so_far[b:e].reshape(a.shape) for a, b, e in zip(arrays, ends, ends[1:])))


def from_behind(shard, axis, by):
    size = lax.axis_size(axis)
    pairs = [(i, i + by) for i in range(size) if 0 <= i + by < size]
    return lax.ppermute(shard, axis, pairs)


def rows_first(arrays, axis, dims):
    turned = [jnp.moveaxis(a, dim, 0) for a, dim in zip(arrays, dims)]
    widths = [t[0].size for t in turned]
    both = jnp.concatenate([t.reshape(-1, w) for t, w in zip(turned, widths)], axis=1)
    filled = lax.all_gather(both, axis, axis=0, tiled=True)
    tiles = jnp.split(filled, [sum(widths[:k]) for k in range(1, len(widths))], axis=1)
    return tuple(
        (
            jnp.moveaxis(b.reshape(-1, *t.shape[1:]), 0, dim)
            for b, t, dim in zip(tiles, turned, dims)
        )
    )


def cut_along(shard, dim, size):
    dims = shard.shape
    tiles = shard.reshape(*dims[:dim], size, dims[dim] // size, *dims[dim + 1 :])
    return jnp.moveaxis(tiles, dim, 0)


def sum_at_owner(shard, axis, dim):
    size = lax.axis_size(axis)
    tiles = lax.all_to_all(cut_along(shard, dim, size), axis, 0, 0, tiled=True)
    return jnp.sum(tiles.astype(jnp.float32), axis=0)


def in_one_piece(arrays, axis, dim, along):
    both = jnp.concatenate(arrays, axis=along)
    filled, at, done = (sum_at_owner(both, axis, dim), 0, [])
    for a in arrays:
        done.append(lax.slice_in_dim(filled, at, at + a.shape[along], axis=along))
        at += a.shape[along]
    return tuple(done)


def sinusoid(time_step):
    half_freq = FREQ // 2
    frequency = jnp.exp(-math.log(10000.0) * jnp.arange(half_freq, dtype=jnp.float32) / half_freq)
    angles = time_step.astype(jnp.float32) * frequency
    return jnp.concatenate([jnp.cos(angles), jnp.sin(angles)]).astype(jnp.bfloat16)


def embed_stats(stacked, embed_table):
    embedded = lax.dot_general(
        stacked, embed_table, (((0,), (0,)), ((), ())), preferred_element_type=jnp.float32
    )
    row_mean = jnp.mean(embedded, axis=1)
    centered = embedded - row_mean[:, None]
    rscale = lax.rsqrt(jnp.mean(centered * centered, axis=1) + norm_floor)
    return (embedded, row_mean, rscale)


def fold_heads(embed_table, modulation, query_proj, key_proj, value_proj):
    scale_row = 1.0 + modulation[1]
    widened = embed_table.astype(jnp.float32) * scale_row[None, :]

    def fold_one(weight):
        wide_weight = weight.astype(jnp.float32)
        main_part = jnp.dot(widened, wide_weight, precision=highest)
        column_sum = jnp.dot(scale_row, wide_weight, precision=highest)
        offset = jnp.dot(modulation[0], wide_weight, precision=highest)
        return jnp.concatenate([main_part, column_sum[None, :], offset[None, :]], axis=0)

    return jnp.stack([fold_one(query_proj), fold_one(key_proj), fold_one(value_proj)])


def project(stacked, row_mean, rscale, folded):
    kin_rows = stacked.shape[0]
    base_part = jnp.einsum(
        "kr,pkc->prc", stacked.astype(jnp.float32), folded[:, :kin_rows], precision=highest
    )
    return (
        rscale[None, :, None] * base_part
        - (rscale * row_mean)[None, :, None] * folded[:, kin_rows][:, None, :]
        + folded[:, kin_rows + 1][:, None, :]
    )


def rms_round(vector, total_sq, columns, gain_row):
    return (
        vector * lax.rsqrt(total_sq / columns + norm_floor)[:, None] * gain_row[None, :]
    ).astype(jnp.bfloat16)


def attend(query_norm, key_norm, value_norm):
    token_count = query_norm.shape[0]
    block_rows = min(512, token_count)
    frames = jnp.arange(token_count, dtype=jnp.int32) // FTOK

    def one_block(row_start):
        query_block = lax.dynamic_slice_in_dim(query_norm, row_start, block_rows, 0)
        scores = jnp.einsum(
            "qhd,khd->hqk", query_block, key_norm, preferred_element_type=jnp.float32
        ) / math.sqrt(HD)
        query_frames = lax.dynamic_slice_in_dim(frames, row_start, block_rows, 0)
        allowed = frames[None, :] <= query_frames[:, None]
        scores = jnp.where(allowed[None], scores, -1e30)
        row_peak = jnp.max(scores, axis=2, keepdims=True)
        exp_scores = jnp.exp(scores - row_peak)
        attn_probs = (exp_scores / jnp.sum(exp_scores, axis=2, keepdims=True)).astype(jnp.bfloat16)
        return jnp.einsum(
            "hqk,khd->qhd", attn_probs, value_norm, preferred_element_type=jnp.float32
        ).astype(jnp.bfloat16)

    starts = jnp.arange(token_count // block_rows, dtype=jnp.int32) * block_rows
    pieces = lax.map(one_block, starts)
    return pieces.reshape(token_count, query_norm.shape[1], query_norm.shape[2])


def head_terms(attended, out_rows, modulation, final_proj):
    gated = out_rows.astype(jnp.float32) * modulation[2][None, :]
    folded_out = lax.dot_general(
        gated, final_proj.astype(jnp.float32), (((1,), (1,)), ((), ())), precision=highest
    )
    flat_heads = attended.reshape(attended.shape[0], -1).astype(jnp.float32)
    return lax.dot_general(folded_out, flat_heads, (((0,), (1,)), ((), ())), precision=highest)


def per_device(
    hidden_states,
    gen_weight,
    noise_field,
    timesteps,
    embed_real,
    time_real,
    query_real,
    key_real,
    value_real,
    out_real,
    gain_real,
    proj_real,
    embed_fake,
    time_fake,
    query_fake,
    key_fake,
    value_fake,
    out_fake,
    gain_fake,
    proj_fake,
):
    devices = lax.axis_size("tm")
    frame_tokens = hidden_states.shape[1]
    tokens = frame_tokens * devices
    patch_rows = gen_weight.shape[0]
    time_step = timesteps[0]
    level_raw = time_step.astype(jnp.float32) / 1000.0
    noise_level = 5.0 * level_raw / (1.0 + 4.0 * level_raw)
    generated = lax.dot_general(
        gen_weight, hidden_states[0], (((1,), (1,)), ((), ())), preferred_element_type=jnp.float32
    ).astype(jnp.bfloat16)
    noisy_patch = (
        (1.0 - noise_level) * generated.astype(jnp.float32)
        + noise_level * noise_field[0].astype(jnp.float32)
    ).astype(jnp.bfloat16)
    sinus_wave = sinusoid(time_step)
    freq_rows = time_real.shape[0]
    own_wave = lax.dynamic_slice_in_dim(sinus_wave, lax.axis_index("tm") * freq_rows, freq_rows, 0)
    share_real = jnp.einsum("f,fcd->cd", own_wave, time_real, preferred_element_type=jnp.float32)
    share_fake = jnp.einsum("f,fcd->cd", own_wave, time_fake, preferred_element_type=jnp.float32)
    modul_real, modul_fake = together((share_real, share_fake), "tm")
    earlier = from_behind(noisy_patch, "tm", 1)
    stacked = jnp.concatenate([noisy_patch, earlier], axis=0)
    embedded_real, mean_real, rscale_real = embed_stats(stacked, embed_real)
    embedded_fake, mean_fake, rscale_fake = embed_stats(stacked, embed_fake)
    folded_real = fold_heads(embed_real, modul_real, query_real, key_real, value_real)
    folded_fake = fold_heads(embed_fake, modul_fake, query_fake, key_fake, value_fake)
    local_width = query_real.shape[1]
    local_heads = local_width // HD
    columns = local_width * devices
    gathered = rows_first(
        (noisy_patch.astype(jnp.float32), mean_real, rscale_real, mean_fake, rscale_fake),
        "tm",
        (1, 0, 0, 0, 0),
    )
    all_patch = gathered[0].astype(jnp.bfloat16)
    prior_frame = jnp.concatenate(
        [
            jnp.zeros((patch_rows, frame_tokens), jnp.bfloat16),
            all_patch[:, : tokens - frame_tokens],
        ],
        axis=1,
    )
    all_stacked = jnp.concatenate([all_patch, prior_frame], axis=0)
    qkv_real = project(all_stacked, gathered[1], gathered[2], folded_real)
    qkv_fake = project(all_stacked, gathered[3], gathered[4], folded_fake)
    norm_sums = together(
        (
            jnp.sum(qkv_real[0] * qkv_real[0], axis=1),
            jnp.sum(qkv_real[1] * qkv_real[1], axis=1),
            jnp.sum(qkv_fake[0] * qkv_fake[0], axis=1),
            jnp.sum(qkv_fake[1] * qkv_fake[1], axis=1),
        ),
        "tm",
    )
    head_shape = (tokens, local_heads, HD)
    attended_real = attend(
        rms_round(qkv_real[0], norm_sums[0], columns, gain_real[0]).reshape(head_shape),
        rms_round(qkv_real[1], norm_sums[1], columns, gain_real[1]).reshape(head_shape),
        qkv_real[2].astype(jnp.bfloat16).reshape(head_shape),
    )
    attended_fake = attend(
        rms_round(qkv_fake[0], norm_sums[2], columns, gain_fake[0]).reshape(head_shape),
        rms_round(qkv_fake[1], norm_sums[3], columns, gain_fake[1]).reshape(head_shape),
        qkv_fake[2].astype(jnp.bfloat16).reshape(head_shape),
    )
    term_real = head_terms(attended_real, out_real, modul_real, proj_real)
    term_fake = head_terms(attended_fake, out_fake, modul_fake, proj_fake)
    own_real, own_fake = in_one_piece(
        (term_real.astype(jnp.bfloat16), term_fake.astype(jnp.bfloat16)), "tm", 1, 0
    )
    velocity_real = own_real + lax.dot_general(
        proj_real.astype(jnp.float32), embedded_real, (((1,), (1,)), ((), ())), precision=highest
    )
    velocity_fake = own_fake + lax.dot_general(
        proj_fake.astype(jnp.float32), embedded_fake, (((1,), (1,)), ((), ())), precision=highest
    )
    pred_real = noisy_patch.astype(jnp.float32) - noise_level * velocity_real
    pred_fake = noisy_patch.astype(jnp.float32) - noise_level * velocity_fake
    gap_local = jnp.sum(jnp.abs(generated.astype(jnp.float32) - pred_real))
    count_all = patch_rows * tokens
    grad_root = math.sqrt(lax.axis_size("batch") * hidden_states.shape[0] * tokens)
    gap_diff = pred_fake - pred_real
    difference = gap_diff.astype(jnp.bfloat16)
    partial_grad = jnp.dot(difference, hidden_states[0], preferred_element_type=jnp.float32)
    gap_total = over_copies(gap_local, "tm")
    normalizer = jnp.maximum(gap_total / count_all, gap_floor)
    weight_grad = lax.psum(partial_grad / normalizer / grad_root, ("tm", "batch"))
    dmd_gradient = (gap_diff / normalizer)[None]
    return (dmd_gradient, weight_grad)


def solution(mesh):
    in_specs = (
        P("batch", "tm", None),
        P(),
        P("batch", None, "tm"),
        P("batch"),
        P(),
        P("tm", None, None),
        P(None, "tm"),
        P(None, "tm"),
        P(None, "tm"),
        P("tm", None),
        P(None, "tm"),
        P(),
        P(),
        P("tm", None, None),
        P(None, "tm"),
        P(None, "tm"),
        P(None, "tm"),
        P("tm", None),
        P(None, "tm"),
        P(),
    )
    out_specs = (P("batch", None, "tm"), P())
    return jax.shard_map(
        per_device, mesh=mesh, in_specs=in_specs, out_specs=out_specs, check_vma=False
    )
```

profile of v0, /device:TPU:1, one launch (start us, length us, event | category | flops | bytes accessed | tf_op | source)
XLA Modules:
  0.0 532.7 jit_solution(16075101230368345085)
XLA Ops:
  10.9 4.6 collective-permute-start
  16.4 2.0 fusion.116
  21.9 3.9 broadcast_in_dim.83
  25.8 8.5 %all-to-all-start = ((f32[32,1,30720]{2,1,0:T(1,128)}), f32[32,1,30720]{2,1,0:T(1,128)}, u32[]{:S(2)}, u32[]{:S(2)}) async-start(f32[32,1,30720]{2,1,0:T(1,128)} %broadcast_in_dim.83), calls=%async_computation | async-start | bytes 7864320 | tf_op jit(solution)/shard_map/all_to_all | solution.py:20
  34.4 58.9 %all-gather.2.cloned.1.call-done = f32[4096,68]{0,1:T(8,128)} async-done(((f32[128,68]{0,1:T(8,128)}), f32[4096,68]{0,1:T(8,128)}) %all-gather.2.cloned.1.call-update) | async-done | bytes 1114128 | tf_op jit(solution)/shard_map/all_gather | solution.py:45
  96.6 4.3 reduce_sum.135
  101.0 3.0 fusion.31
  111.0 1.9 fusion.28
  119.8 3.4 fusion.21
  123.6 2.3 copy-done.7
  125.9 3.6 fusion.20
  129.5 2.6 copy-done.6
  132.5 3.2 broadcast_in_dim.96
  135.7 5.3 all-to-all-start.1
  141.0 2.7 fusion.70
  143.7 2.3 copy.62
  146.0 2.7 fusion.71
  148.6 2.3 copy.65
  150.9 3.8 fusion.32
  154.7 3.8 fusion.23
  158.6 10.8 %all-to-all-done.1 = f32[32,1,16384]{2,1,0:T(1,128)S(1)} async-done(((f32[32,1,16384]{2,1,0:T(1,128)}), f32[32,1,16384]{2,1,0:T(1,128)S(1)}, u32[]{:S(2)}, u32[]{:S(2)}) %all-to-all-start.1) | async-done | bytes 2097184 | tf_op jit(solution)/shard_map/all_to_all | solution.py:20
  170.7 3.8 fusion.40
  175.9 77.0 %while.22 = (s32[]{:T(128)}, bf16[8,512,1,128]{3,1,2,0:T(8,128)(2,1)S(1)}, s32[4096]{0:T(1024)S(1)}, s32[8]{0:T(128)S(1)}, bf16[4096,1,128]{0,2,1:T(8,128)(2,1)}...) while((s32[]{:T(128)}, ...), condition=%wide.region_13.14_spmd.clone, body=%wide.region_10.13_spmd.clone.sunk | while | flops 1092680704 | bytes 31752380 | solution.py:146
  178.3 3.7 fusion.183
  183.3 2.2 fusion.185
  188.0 3.7 fusion.183
  192.9 2.2 fusion.185
  197.6 3.7 fusion.183
  202.6 2.2 fusion.185
  207.2 3.7 fusion.183
  212.2 2.2 fusion.185
  216.8 3.7 fusion.183
  221.8 2.2 fusion.185
  226.5 3.7 fusion.183
  231.4 2.2 fusion.185
  236.1 3.7 fusion.183
  241.1 2.2 fusion.185
  245.7 3.7 fusion.183
  250.7 2.2 fusion.185
  252.9 3.8 fusion.36
  258.1 77.3 %while.23 = (s32[]{:T(128)}, bf16[8,512,1,128]{3,1,2,0:T(8,128)(2,1)S(1)}, s32[4096]{0:T(1024)S(1)}, s32[8]{0:T(128)S(1)}, bf16[4096,1,128]{0,2,1:T(8,128)(2,1)}...) while((s32[]{:T(128)}, ...), condition=%wide.region_17.18_spmd.clone, body=%wide.region_14.17_spmd.clone.sunk | while | flops 1092680704 | bytes 31752380 | solution.py:146
  260.8 3.7 fusion.187
  265.7 2.2 fusion.189
  270.4 3.7 fusion.187
  275.4 2.2 fusion.189
  280.0 3.7 fusion.187
  285.0 2.2 fusion.189
  289.7 3.7 fusion.187
  294.6 2.2 fusion.189
  299.3 3.7 fusion.187
  304.3 2.2 fusion.189
  308.9 3.7 fusion.187
  313.9 2.2 fusion.189
  318.6 3.7 fusion.187
  323.5 2.2 fusion.189
  328.2 3.6 fusion.187
  333.1 2.2 fusion.189
  338.2 20.8 %all_to_all.23 = bf16[32,128,128]{2,1,0:T(8,128)(2,1)S(1)} all-to-all(bf16[32,128,128]{2,1,0:T(8,128)(2,1)S(1)} %bitcast_bitcast_fusion), channel_id=1, replica_groups=mesh['tm'=32,'batch'=4] {'tm'}, dimensions={0} | all-to-all | bytes 2097152 | tf_op jit(solution)/shard_map/all_to_all | solution.py:63
  359.1 2.3 abs_reduce_fusion
  362.7 3.9 all-to-all-start.3
  366.7 3.4 fusion.59
  370.1 3.4 all-to-all-done.3
  376.8 146.3 %all-reduce.3.cloned.1.call-done = f32[64,5120]{1,0:T(8,128)} async-done(((f32[64,5120]{1,0:T(8,128)}), f32[64,5120]{1,0:T(8,128)}) %all-reduce.3.cloned.1.call-update) | async-done | bytes 1310736 | tf_op jit(solution)/shard_map/psum | solution.py:267
  523.2 2.5 copy.121
  (213 shorter events, 67.3 us)
Async XLA Ops:
  7.2 1.3 copy-start
  7.2 8.4 %copy-start.23 = (bf16[8,3,5120]{2,0,1:T(8,128)(2,1)S(1)}, bf16[8,3,5120]{2,0,1:T(8,128)(2,1)}, u32[]{:S(2)}) copy-start(bf16[8,3,5120]{2,0,1:T(8,128)(2,1)} %param.29) | copy-start | bytes 737284
  7.2 8.7 %copy-start.24 = (bf16[8,3,5120]{2,0,1:T(8,128)(2,1)S(1)}, bf16[8,3,5120]{2,0,1:T(8,128)(2,1)}, u32[]{:S(2)}) copy-start(bf16[8,3,5120]{2,0,1:T(8,128)(2,1)} %param.37) | copy-start | bytes 737284
  7.2 86.1 %all-gather.2.cloned.1.call-start = ((), (), s32[]{:S(2)}) async-start(), calls=%async_computation.4 | async-start | bytes 1216512 | tf_op jit(solution)/shard_map/all_gather | solution.py:45
  10.2 0.8 copy-start.21
  10.9 7.5 %copy-start.19 = (bf16[64,128]{1,0:T(8,128)(2,1)}, bf16[64,128]{1,0:T(8,128)(2,1)S(1)}, u32[]{:S(2)}) copy-start(bf16[64,128]{1,0:T(8,128)(2,1)S(1)} %get-tuple-element.223) | copy-start | bytes 49156
  10.9 5.4 %collective-permute-start = (bf16[64,128]{1,0:T(8,128)(2,1)S(1)}, bf16[64,128]{1,0:T(8,128)(2,1)S(1)}, u32[]{:S(2)}, u32[]{:S(2)}) collective-permute-start(bf16[64,128]{1,0:T(8,128)(2,1)S(1)} %get-tuple-element.223), channel_id=1, source_target_pairs={{0,4},{4,8},{8,12},{12,16},{16,20},{20,24},{24,28},{28,32},{32,36}... | collective-permute-start | bytes 49160 | tf_op jit(solution)/shard_map/ppermute | solution.py:38
  16.3 2.2 copy-start.4
  18.4 1.5 copy-start.1
  19.0 1.6 copy-start.2
  25.8 8.5 %copy-start.27 = (f32[2,128]{1,0:T(2,128)S(1)}, f32[2,128]{1,0:T(2,128)}, u32[]{:S(2)}) copy-start(f32[2,128]{1,0:T(2,128)} %param.34) | copy-start | bytes 3076
  25.8 8.5 %copy-start.28 = (f32[2,128]{1,0:T(2,128)S(1)}, f32[2,128]{1,0:T(2,128)}, u32[]{:S(2)}) copy-start(f32[2,128]{1,0:T(2,128)} %param.42) | copy-start | bytes 3076
  25.8 70.8 %all-to-all-start = ((f32[32,1,30720]{2,1,0:T(1,128)}), f32[32,1,30720]{2,1,0:T(1,128)}, u32[]{:S(2)}, u32[]{:S(2)}) async-start(f32[32,1,30720]{2,1,0:T(1,128)} %broadcast_in_dim.83), calls=%async_computation | async-start | bytes 7864320 | tf_op jit(solution)/shard_map/all_to_all | solution.py:20
  101.0 3.0 copy-start.8
  101.0 3.6 copy-start.9
  105.3 2.8 copy-start.10
  108.7 2.3 copy-start.5
  108.7 2.3 copy-start.11
  110.9 2.6 copy-start.12
  114.2 2.8 copy-start.13
  117.6 2.3 copy-start.18
  123.2 2.7 copy-start.7
  129.4 2.7 copy-start.6
  135.7 33.7 %all-to-all-start.1 = ((f32[32,1,16384]{2,1,0:T(1,128)}), f32[32,1,16384]{2,1,0:T(1,128)S(1)}, u32[]{:S(2)}, u32[]{:S(2)}) async-start(f32[32,1,16384]{2,1,0:T(1,128)} %broadcast_in_dim.96), calls=%async_computation.1 | async-start | bytes 4194304 | tf_op jit(solution)/shard_map/all_to_all | solution.py:20
  182.0 1.3 copy-start.17
  191.6 1.3 copy-start.17
  201.3 1.3 copy-start.17
  210.9 1.3 copy-start.17
  220.5 1.3 copy-start.17
  230.1 1.3 copy-start.17
  239.8 1.3 copy-start.17
  249.4 1.3 copy-start.17
  258.1 77.3 %copy-start.26 = (f32[128,64]{0,1:T(8,128)S(1)}, f32[128,64]{0,1:T(8,128)}, u32[]{:S(2)}) copy-start(f32[128,64]{0,1:T(8,128)} %fusion.32) | copy-start | bytes 98308
  258.1 78.5 %copy-start.25 = (f32[128,64]{0,1:T(8,128)S(1)}, f32[128,64]{0,1:T(8,128)}, u32[]{:S(2)}) copy-start(f32[128,64]{0,1:T(8,128)} %fusion.23) | copy-start | bytes 98308
  264.4 1.3 copy-start.16
  274.1 1.3 copy-start.16
  283.7 1.3 copy-start.16
  293.3 1.3 copy-start.16
  303.0 1.3 copy-start.16
  312.6 1.3 copy-start.16
  322.2 1.3 copy-start.16
  331.8 1.3 copy-start.16
  337.8 21.3 %copy-start.14 = (bf16[64,5120]{1,0:T(8,128)(2,1)S(1)}, bf16[64,5120]{1,0:T(8,128)(2,1)}, u32[]{:S(2)}) copy-start(bf16[64,5120]{1,0:T(8,128)(2,1)} %param.35) | copy-start | bytes 1966084
  338.1 21.0 %copy-start.3 = (f32[128,5120]{1,0:T(8,128)S(1)}, f32[128,5120]{1,0:T(8,128)}, u32[]{:S(2)}) copy-start(f32[128,5120]{1,0:T(8,128)} %copy-done.2) | copy-start | bytes 7864324
  338.1 21.0 %copy-start.20 = (bf16[64,128]{1,0:T(8,128)(2,1)S(1)}, bf16[64,128]{1,0:T(8,128)(2,1)}, u32[]{:S(2)}) copy-start(bf16[64,128]{1,0:T(8,128)(2,1)} %copy-done.19) | copy-start | bytes 49156
  338.1 21.0 %copy-start.22 = (f32[64,128]{1,0:T(8,128)S(1)}, f32[64,128]{1,0:T(8,128)}, u32[]{:S(2)}) copy-start(f32[64,128]{1,0:T(8,128)} %copy-done.21) | copy-start | bytes 98308
  358.9 7.7 %copy-start.15 = (bf16[64,5120]{1,0:T(8,128)(2,1)S(1)}, bf16[64,5120]{1,0:T(8,128)(2,1)}, u32[]{:S(2)}) copy-start(bf16[64,5120]{1,0:T(8,128)(2,1)} %param.43) | copy-start | bytes 1966084
  362.7 10.8 %all-to-all-start.3 = ((f32[32,1,1]{2,1,0:T(1,128)}), f32[32,1,1]{2,1,0:T(1,128)S(1)}, u32[]{:S(2)}, u32[]{:S(2)}) async-start(f32[32,1,1]{2,1,0:T(1,128)} %broadcast_in_dim.97), calls=%async_computation.3 | async-start | bytes 32768 | tf_op jit(solution)/shard_map/all_to_all | solution.py:20
  366.6 156.6 %all-reduce.3.cloned.1.call-start = ((), (), s32[]{:S(2)}) async-start(), calls=%async_computation.5 | async-start | bytes 2621440 | tf_op jit(solution)/shard_map/psum | solution.py:267
Sparse Core Ops, SparseCore 0:
  22.0 71.2 all-gather.1
  376.3 146.7 all-reduce.2
where the time goes:
time: 539 us; the launch traced here: 533 us
  waiting for transfers between devices  220 us (41%)
  matrix products  142 us (26%)
  local copies, waits for them, and re-layouts  45.3 us (8%)
  other arithmetic  37.9 us (7%)
  loops' own time  28.4 us (5%)
  starting transfers between devices  22.4 us (4%)
  blocking collectives  20.8 us (4%)
  between operations  16.4 us (3%)
    psum x1, waiting for transfers between devices, per_device(): lax.psum(partial_grad / normalizer / grad_root, ('tm', 'batch'))  146 us
    all_gather x1, waiting for transfers between devices, rows_first(): filled = lax.all_gather(both, axis, axis=0, tiled=True)  58.9 us
    dot_general x16, matrix products, one_block(): jnp.einsum('qhd,khd->hqk', query_block, key_norm, preferred_element_type=...  58.7 us
    dot_general x16, matrix products, one_block(): jnp.einsum('hqk,khd->qhd', attn_probs, value_norm, preferred_element_type...  35.9 us
    another operation x2, loops' own time, attend(): pieces = lax.map(one_block, starts)  28.4 us
    all_to_all x1, blocking collectives, sum_at_owner(): tiles = lax.all_to_all(cut_along(shard, dim, size), axis, 0, 0, tiled=True)  20.8 us
    reduce_sum x16, other arithmetic, one_block(): jnp.sum(exp_scores, axis=2, keepdims=True)  20.4 us
    all_to_all x3, starting transfers between devices, copy_for_each(): return lax.all_to_all(copies, axis, split_axis=0, concat_axis=0, tiled=True)  17.7 us
  transfers between devices with their start and end apart: 6, of which 4 were waited for; matrix products, arithmetic and copies ran while one was open for 6% of the time, Pallas kernels for 0%

commit v1 on v0

v1 whole, which is shorter than its diff:
```python
import functools
import math

import jax
import jax.numpy as jnp
from jax import lax
from jax.experimental import pallas as pl
from jax.experimental.pallas import tpu as pltpu
from jax.sharding import PartitionSpec as P

HD = 128
FREQ = 256
FT = 128
MESH = pl.DeviceIdType.MESH

norm_floor = 0.05
gap_floor = 0.25
highest = lax.Precision.HIGHEST
f32 = jnp.float32
bf16 = jnp.bfloat16


def split2(a):
    hi = a.astype(bf16)
    lo = (a - hi.astype(f32)).astype(bf16)
    return hi, lo


def stack2(a):
    hi, lo = split2(a)
    return jnp.concatenate([hi, lo], axis=0)


def mm(a, b):
    return jnp.dot(a, b, preferred_element_type=f32)


def mm_t(a, b):
    return lax.dot_general(a, b, (((1,), (1,)), ((), ())), preferred_element_type=f32)


def attend_block(block, blk, qt_ref, k_ref, v_ref, m_ref, o_ref):
    q_at = pl.multiple_of(block * blk, blk)
    frames = blk // FT

    def tile(net, k_at, diagonal):
        s = mm(k_ref[net, pl.ds(k_at, blk), :], qt_ref[net, :, pl.ds(q_at, blk)])
        if diagonal:
            rows = []
            for r in range(frames):
                part = s[r * FT : (r + 1) * FT]
                if r:
                    gone = jnp.full((FT, r * FT), -1e30, f32)
                    part = jnp.concatenate([gone, part[:, r * FT :]], axis=1)
                rows.append(part)
            s = jnp.concatenate(rows, axis=0)
        return s

    for net in range(2):
        s = tile(net, q_at, True)
        top = jnp.max(s, axis=0, keepdims=True)
        p = jnp.exp2(s - top).astype(bf16)
        m_ref[net] = jnp.broadcast_to(top, (8, blk))
        o_ref[net] = mm(v_ref[net, :, pl.ds(q_at, blk)], p)

    def step(kb, _):
        k_at = pl.multiple_of(kb * blk, blk)
        ss = [tile(net, k_at, False) for net in range(2)]
        for net in range(2):
            s = ss[net]
            old = m_ref[net, 0:1, :]
            top = jnp.maximum(old, jnp.max(s, axis=0, keepdims=True))
            p = jnp.exp2(s - top).astype(bf16)
            fade = jnp.exp2(old - top)
            m_ref[net] = jnp.broadcast_to(top, (8, blk))
            o_ref[net] = o_ref[net] * fade + mm(v_ref[net, :, pl.ds(k_at, blk)], p)
        return 0

    lax.fori_loop(0, block, step, 0)


def kernel(
    n, nz, blk,
    sc, noise, time_r, time_f, gain_r, gain_f,
    hidden_h, genw_h, emb_rh, emb_fh, proj_rh, proj_fh, out_rh, out_fh,
    wq_r, wk_r, wv_r, wq_f, wk_f, wv_f,
    dmd_ref, wg_ref,
    hid, genw, emb, proj, outw, wqk, wv,
    modbuf, modin, modfull, xg, xs, gen_s, mu_s, gmat, rmat,
    lhs, acc, lhs2, acc2, accv, rs_s, qraw, kraw, nbuf, nin, nfull,
    qt, kn, vt, m_s, o_s,
    tsend, trecv, gapbuf, wsend, wrecv, zbuf,
    lsem, s_mod, r_mod, s_mod2, r_mod2, s_x, r_x, s_n, r_n, s_n2, r_n2,
    s_t, r_t, s_g, r_g, s_w, r_w, s_z, r_z, s_a, r_a,
):
    me = lax.axis_index("tm")
    mz = lax.axis_index("batch")
    d = hid.shape[1]
    groups = d // 1024
    tokens = n * FT

    loads = []

    def load(src, dst):
        c = pltpu.make_async_copy(src, dst, lsem.at[len(loads)])
        c.start()
        loads.append(c)
        return c

    ld_hid = load(hidden_h.at[0], hid)
    ld_gen = load(genw_h, genw)
    ld_emb = [load(emb_rh, emb.at[0]), load(emb_fh, emb.at[1])]
    ld_proj = [load(proj_rh, proj.at[0]), load(proj_fh, proj.at[1])]
    ld_qk = []
    for net, (a, b) in enumerate(((wq_r, wk_r), (wq_f, wk_f))):
        ld_qk.append(load(a, wqk.at[net, :, 0:HD]))
        ld_qk.append(load(b, wqk.at[net, :, HD : 2 * HD]))
    ld_v = [load(wv_r, wv.at[0]), load(wv_f, wv.at[1])]
    ld_out = [load(out_rh, outw.at[0]), load(out_fh, outw.at[1])]

    barrier = pltpu.get_barrier_semaphore()

    def greet(i, _):
        pl.semaphore_signal(
            barrier, inc=1, device_id={"tm": lax.rem(me + i, n)}, device_id_type=MESH
        )
        return 0

    lax.fori_loop(1, n, greet, 0)
    for i in range(1, nz):
        pl.semaphore_signal(
            barrier, inc=1, device_id={"batch": lax.rem(mz + i, nz)}, device_id_type=MESH
        )

    def rc(src, dst, ssem, rsem, j):
        return pltpu.make_async_remote_copy(
            src_ref=src, dst_ref=dst, send_sem=ssem, recv_sem=rsem,
            device_id={"tm": j}, device_id_type=MESH,
        )

    def spread(src_of, dst_of, ss, rr):
        def body(i, _):
            j = lax.rem(me + i, n)
            rc(src_of(j), dst_of(me), ss.at[i], rr.at[i], j).start()
            return 0

        lax.fori_loop(1, n, body, 0)

    def collect(src_of, dst_of, ss, rr):
        def body(i, _):
            j = lax.rem(me + i, n)
            frm = lax.rem(me + n - i, n)
            c = rc(src_of(j), dst_of(frm), ss.at[i], rr.at[i], j)
            c.wait_recv()
            c.wait_send()
            return 0

        lax.fori_loop(1, n, body, 0)

    for p in range(6 * groups, n):
        modbuf[p] = jnp.zeros((8, 128), f32)
    for net, table in enumerate((time_r, time_f)):
        for g in range(groups):
            part = None
            for f in range(table.shape[0]):
                term = sc[8 + f] * table[f, :, g * 1024 : (g + 1) * 1024].astype(f32)
                part = term if part is None else part + term
            for c in range(3):
                for r in range(8):
                    modbuf[(net * 3 + c) * groups + g, r : r + 1, :] = part[
                        c : c + 1, r * 128 : (r + 1) * 128
                    ]
    modin[me] = modbuf[me]
    pl.semaphore_wait(barrier, n - 1 + nz - 1)
    spread(lambda j: modbuf.at[j], lambda s: modin.at[s], s_mod, r_mod)

    ld_hid.wait()
    ld_gen.wait()
    generated = mm_t(genw[...], hid[...]).astype(bf16)
    gen_s[...] = generated
    xg[0] = jnp.zeros(xg.shape[1:], bf16)
    xg[me + 1] = (sc[1] * generated.astype(f32) + sc[0] * noise[0].astype(f32)).astype(bf16)
    spread(lambda j: xg.at[me + 1], lambda s: xg.at[s + 1], s_x, r_x)

    for net in range(2):
        ld_emb[net].wait()
        ld_proj[net].wait()

        def total(g, t):
            at = pl.multiple_of(g * 1024, 1024)
            return t + jnp.sum(emb[net, :, pl.ds(at, 1024)].astype(f32), axis=1, keepdims=True)

        mu = lax.fori_loop(0, groups, total, jnp.zeros((128, 1), f32)) / d
        mu_s[net] = jnp.broadcast_to(mu, (128, 128))

        def gram(g, t):
            at = pl.multiple_of(g * 1024, 1024)
            e = emb[net, :, pl.ds(at, 1024)]
            hi, lo = split2(e.astype(f32) - mu)
            both = jnp.concatenate([hi, lo], axis=0)
            return t[0] + mm_t(both, hi), t[1] + mm_t(proj[net, :, pl.ds(at, 1024)], e)

        gg, rr = lax.fori_loop(
            0, groups, gram, (jnp.zeros((256, 128), f32), jnp.zeros((64, 128), f32))
        )
        lh = gg[128:256]
        gmat[net] = stack2((gg[0:128] + lh + lh.T) / d)
        rmat[net] = stack2(rr)

    collect(lambda j: modbuf.at[j], lambda s: modin.at[s], s_mod, r_mod)
    modfull[me] = jnp.sum(modin[...], axis=0)
    spread(lambda j: modfull.at[me], lambda s: modfull.at[s], s_mod2, r_mod2)

    collect(lambda j: xg.at[me + 1], lambda s: xg.at[s + 1], s_x, r_x)

    def place(j, _):
        at = pl.multiple_of(j * FT, FT)
        xs[0:64, pl.ds(at, FT)] = xg[j + 1]
        xs[64:128, pl.ds(at, FT)] = xg[j]
        return 0

    lax.fori_loop(0, n, place, 0)

    width = blk

    def variances(t, _):
        at = pl.multiple_of(t * width, width)
        x = xs[:, pl.ds(at, width)]
        for net in range(2):
            y = mm(gmat[net], x)
            var = jnp.sum((y[0:128] + y[128:256]) * x.astype(f32), axis=0, keepdims=True)
            rs = lax.rsqrt(jnp.maximum(var, 0.0) + norm_floor)
            rs_s[net, :, pl.ds(at, width)] = jnp.broadcast_to(rs, (8, width))
        return 0

    lax.fori_loop(0, tokens // width, variances, 0)

    collect(lambda j: modfull.at[me], lambda s: modfull.at[s], s_mod2, r_mod2)

    for c in ld_qk:
        c.wait()
    row = lax.broadcasted_iota(jnp.int32, (16, 128), 0)
    for net in range(2):
        acc[...] = jnp.zeros_like(acc)

        def fold(g, _):
            at = pl.multiple_of(g * 1024, 1024)
            shift8 = modfull[(net * 3 + 0) * groups + g]
            scale8 = modfull[(net * 3 + 1) * groups + g]
            for r in range(8):
                col = pl.multiple_of(at + r * 128, 128)
                e = emb[net, :, pl.ds(col, 128)].astype(f32) - mu_s[net]
                hi, lo = split2(e * (1.0 + scale8[r : r + 1, :]))
                sh, sl = split2(shift8[r : r + 1, :])
                lhs[net, 0:128, pl.ds(col, 128)] = hi
                lhs[net, 128:256, pl.ds(col, 128)] = lo
                tail = jnp.where(
                    row == 0, sh.astype(f32), jnp.where(row == 1, sl.astype(f32), 0.0)
                )
                lhs[net, 256:272, pl.ds(col, 128)] = tail.astype(bf16)
            acc[...] += mm(lhs[net, :, pl.ds(at, 1024)], wqk[net, pl.ds(at, 1024), :])
            return 0

        lax.fori_loop(0, groups, fold, 0)
        a = acc[0:128, :] + acc[128:256, :]
        off = acc[256:257, :] + acc[257:258, :]
        a_q = stack2(a[:, 0:HD].T)
        a_k = stack2(a[:, HD : 2 * HD].T)
        off_q = jnp.broadcast_to(off[:, 0:HD], (128, 128)).T[:, 0:1]
        off_k = jnp.broadcast_to(off[:, HD : 2 * HD], (128, 128)).T[:, 0:1]

        def project(t, _):
            at = pl.multiple_of(t * width, width)
            x = xs[:, pl.ds(at, width)]
            rs = rs_s[net, 0:1, pl.ds(at, width)]
            for which, (mat, off_c, dst) in enumerate(((a_q, off_q, qraw), (a_k, off_k, kraw))):
                y = mm(mat, x)
                y = (y[0:128] + y[128:256]) * rs + off_c
                dst[net, :, pl.ds(at, width)] = y
                sq = jnp.sum(y * y, axis=0, keepdims=True)
                for r in range(width // FT):
                    nbuf[t * (width // FT) + r, net * 2 + which : net * 2 + which + 1, :] = sq[
                        :, r * FT : (r + 1) * FT
                    ]
            return 0

        lax.fori_loop(0, tokens // width, project, 0)

    nin[me] = nbuf[me]
    spread(lambda j: nbuf.at[j], lambda s: nin.at[s], s_n, r_n)

    for c in ld_v + ld_out:
        c.wait()
    for net in range(2):
        accv[...] = jnp.zeros_like(accv)
        acc2[...] = jnp.zeros_like(acc2)

        def fold_v(g, _):
            at = pl.multiple_of(g * 1024, 1024)
            gate8 = modfull[(net * 3 + 2) * groups + g]
            for r in range(8):
                col = pl.multiple_of(at + r * 128, 128)
                hi, lo = split2(proj[net, :, pl.ds(col, 128)].astype(f32) * gate8[r : r + 1, :])
                lhs2[0:64, r * 128 : (r + 1) * 128] = hi
                lhs2[64:128, r * 128 : (r + 1) * 128] = lo
            accv[...] += mm(lhs[net, :, pl.ds(at, 1024)], wv[net, pl.ds(at, 1024), :])
            acc2[...] += mm_t(lhs2[...], outw[net, :, pl.ds(at, 1024)])
            return 0

        lax.fori_loop(0, groups, fold_v, 0)
        a = accv[0:128, :] + accv[128:256, :]
        off = accv[256:257, :] + accv[257:258, :]
        out_t = acc2[0:64, :] + acc2[64:128, :]
        b_mat = stack2(
            lax.dot_general(
                out_t, a, (((1,), (1,)), ((), ())), precision=highest, preferred_element_type=f32
            )
        )
        off_v = jnp.sum(out_t * off, axis=1, keepdims=True)
        ones = jnp.where(lax.broadcasted_iota(jnp.int32, (16, width), 0) == 0, 1.0, 0.0)

        def values(t, _):
            at = pl.multiple_of(t * width, width)
            y = mm(b_mat, xs[:, pl.ds(at, width)])
            y = (y[0:64] + y[64:128]) * rs_s[net, 0:1, pl.ds(at, width)] + off_v
            vt[net, 0:64, pl.ds(at, width)] = y.astype(bf16)
            vt[net, 64:80, pl.ds(at, width)] = ones.astype(bf16)
            return 0

        lax.fori_loop(0, tokens // width, values, 0)

    collect(lambda j: nbuf.at[j], lambda s: nin.at[s], s_n, r_n)
    nfull[me] = lax.rsqrt(jnp.sum(nin[...], axis=0) / tokens_cols(n) + norm_floor)
    spread(lambda j: nfull.at[me], lambda s: nfull.at[s], s_n2, r_n2)
    collect(lambda j: nfull.at[me], lambda s: nfull.at[s], s_n2, r_n2)

    for net, gain in enumerate((gain_r, gain_f)):
        both = gain[0:1, :] * gain[1:2, :] * (math.log2(math.e) / math.sqrt(HD))
        g_col = jnp.broadcast_to(both, (128, 128)).T

        def normalise(j, _):
            at = pl.multiple_of(j * FT, FT)
            sq = nfull[j, net * 2 : net * 2 + 1, :]
            sk = nfull[j, net * 2 + 1 : net * 2 + 2, :]
            qt[net, :, pl.ds(at, FT)] = (qraw[net, :, pl.ds(at, FT)] * sq * g_col).astype(bf16)
            kn[net, pl.ds(at, FT), :] = (kraw[net, :, pl.ds(at, FT)] * sk).T.astype(bf16)
            return 0

        lax.fori_loop(0, n, normalise, 0)

    blocks = tokens // blk
    per = blk // FT

    def t_copy(f):
        return rc(tsend.at[f], trecv.at[me], s_t.at[f], r_t.at[me], f)

    def one_block(s, _):
        block = lax.rem(s + me, blocks)
        attend_block(block, blk, qt, kn, vt, m_s, o_s)
        for net in range(2):
            o = o_s[net]
            y = (o[0:64] / o[64:65]).astype(bf16)
            for r in range(per):
                tsend[block * per + r, net * 64 : (net + 1) * 64, :] = y[:, r * FT : (r + 1) * FT]
        for r in range(per):
            f = block * per + r

            @pl.when(f != me)
            def _():
                t_copy(f).start()

        return 0

    lax.fori_loop(0, blocks, one_block, 0)
    trecv[me] = tsend[me]

    def t_wait(i, _):
        frm = lax.rem(me + n - i, n)
        f = lax.rem(me + i, n)
        rc(tsend.at[f], trecv.at[frm], s_t.at[f], r_t.at[frm], f).wait_recv()
        t_copy(f).wait_send()
        return 0

    lax.fori_loop(1, n, t_wait, 0)

    def add_up(s, t):
        return t + trecv[s].astype(f32)

    vel = lax.fori_loop(0, n, add_up, jnp.zeros((128, FT), f32))
    x_own = jnp.concatenate([xg[me + 1], xg[me]], axis=0)
    base_r = mm(rmat[0], x_own)
    base_f = mm(rmat[1], x_own)
    vel_r = vel[0:64] + base_r[0:64] + base_r[64:128]
    vel_f = vel[64:128] + base_f[0:64] + base_f[64:128]
    noisy = xg[me + 1].astype(f32)
    pred_r = noisy - sc[0] * vel_r
    pred_f = noisy - sc[0] * vel_f
    gap = jnp.abs(gen_s[...].astype(f32) - pred_r)
    gsum = gap[0:8]
    for r in range(1, 8):
        gsum = gsum + gap[r * 8 : (r + 1) * 8]
    gapbuf[me] = gsum
    spread(lambda j: gapbuf.at[me], lambda s: gapbuf.at[s], s_g, r_g)
    diff = pred_f - pred_r
    diff_b = diff.astype(bf16)

    def wg_part(g, _):
        at = pl.multiple_of(g * 1024, 1024)
        y = mm(diff_b, hid[:, pl.ds(at, 1024)]).astype(bf16)
        for r in range(8):
            to = pl.multiple_of((g * 8 + r) * 64, 64)
            wsend[pl.ds(to, 64), :] = y[:, r * 128 : (r + 1) * 128]
        return 0

    lax.fori_loop(0, groups, wg_part, 0)
    rows = wsend.shape[0] // n

    def w_src(j):
        return wsend.at[pl.ds(pl.multiple_of(j * rows, 16), rows), :]

    spread(w_src, lambda s: wrecv.at[s], s_w, r_w)
    wrecv[me] = wsend[pl.ds(pl.multiple_of(me * rows, 16), rows), :]
    collect(lambda j: gapbuf.at[me], lambda s: gapbuf.at[s], s_g, r_g)
    gap_all = jnp.sum(jnp.sum(gapbuf[...], axis=0), keepdims=True)
    inv = 1.0 / jnp.maximum(gap_all / (64.0 * tokens), gap_floor)
    dmd_ref[0] = diff * inv
    collect(w_src, lambda s: wrecv.at[s], s_w, r_w)

    def add_w(s, t):
        return t + wrecv[s].astype(f32)

    wsum = lax.fori_loop(0, n, add_w, jnp.zeros((rows, 128), f32))
    zbuf[mz] = (wsum * (inv / math.sqrt(nz * tokens))).astype(bf16)

    def zc(i, frm):
        j = lax.rem(mz + i, nz)
        return pltpu.make_async_remote_copy(
            src_ref=zbuf.at[mz], dst_ref=zbuf.at[frm], send_sem=s_z.at[i], recv_sem=r_z.at[i],
            device_id={"batch": j}, device_id_type=MESH,
        )

    for i in range(1, nz):
        zc(i, mz).start()
    for i in range(1, nz):
        c = zc(i, lax.rem(mz + nz - i, nz))
        c.wait_recv()
        c.wait_send()
    whole = zbuf[0].astype(f32)
    for z in range(1, nz):
        whole = whole + zbuf[z].astype(f32)
    wg_ref[me] = whole.astype(bf16)
    spread(lambda j: wg_ref.at[me], lambda s: wg_ref.at[s], s_a, r_a)
    collect(lambda j: wg_ref.at[me], lambda s: wg_ref.at[s], s_a, r_a)


def tokens_cols(n):
    return float(n * HD)


def per_device(
    hidden_states, gen_weight, noise_field, timesteps,
    embed_real, time_real, query_real, key_real, value_real, out_real, gain_real, proj_real,
    embed_fake, time_fake, query_fake, key_fake, value_fake, out_fake, gain_fake, proj_fake,
):
    n = lax.axis_size("tm")
    nz = lax.axis_size("batch")
    d = hidden_states.shape[2]
    tokens = n * FT
    blk = 512
    rows = 64 * d // 128 // n
    fr = time_real.shape[0]
    step = timesteps[0].astype(f32)
    raw = step / 1000.0
    sigma = 5.0 * raw / (1.0 + 4.0 * raw)
    half = FREQ // 2
    at = lax.axis_index("tm") * fr + jnp.arange(fr, dtype=jnp.int32)
    freq = jnp.exp(-math.log(10000.0) * (at % half).astype(f32) / half)
    wave = jnp.where(at < half, jnp.cos(step * freq), jnp.sin(step * freq))
    wave = wave.astype(bf16).astype(f32)
    slot = jnp.arange(8)
    head = jnp.where(slot == 0, sigma, jnp.where(slot == 1, 1.0 - sigma, 0.0))
    sc = jnp.concatenate([head, wave])

    vm = pl.BlockSpec(memory_space=pltpu.VMEM)
    hbm = pl.BlockSpec(memory_space=pl.ANY)
    sems = pltpu.SemaphoreType.DMA
    nb = tokens // blk
    scratch = [
        pltpu.VMEM((FT, d), bf16),
        pltpu.VMEM((64, d), bf16),
        pltpu.VMEM((2, 128, d), bf16),
        pltpu.VMEM((2, 64, d), bf16),
        pltpu.VMEM((2, 128, d), bf16),
        pltpu.VMEM((2, d, 256), bf16),
        pltpu.VMEM((2, d, 128), bf16),
        pltpu.VMEM((n, 8, 128), f32),
        pltpu.VMEM((n, 8, 128), f32),
        pltpu.VMEM((n, 8, 128), f32),
        pltpu.VMEM((n + 1, 64, 128), bf16),
        pltpu.VMEM((128, tokens), bf16),
        pltpu.VMEM((64, 128), bf16),
        pltpu.VMEM((2, 128, 128), f32),
        pltpu.VMEM((2, 256, 128), bf16),
        pltpu.VMEM((2, 128, 128), bf16),
        pltpu.VMEM((2, 272, d), bf16),
        pltpu.VMEM((272, 256), f32),
        pltpu.VMEM((128, 1024), bf16),
        pltpu.VMEM((128, 128), f32),
        pltpu.VMEM((272, 128), f32),
        pltpu.VMEM((2, 8, tokens), f32),
        pltpu.VMEM((2, 128, tokens), f32),
        pltpu.VMEM((2, 128, tokens), f32),
        pltpu.VMEM((n, 8, 128), f32),
        pltpu.VMEM((n, 8, 128), f32),
        pltpu.VMEM((n, 8, 128), f32),
        pltpu.VMEM((2, 128, tokens), bf16),
        pltpu.VMEM((2, tokens, 128), bf16),
        pltpu.VMEM((2, 80, tokens), bf16),
        pltpu.VMEM((2, 8, blk), f32),
        pltpu.VMEM((2, 80, blk), f32),
        pltpu.VMEM((n, 128, 128), bf16),
        pltpu.VMEM((n, 128, 128), bf16),
        pltpu.VMEM((n, 8, 128), f32),
        pltpu.VMEM((rows * n, 128), bf16),
        pltpu.VMEM((n, rows, 128), bf16),
        pltpu.VMEM((nz, rows, 128), bf16),
        sems((16,)),
    ] + [sems((n,)) for _ in range(20)]
    dmd, wg = pl.pallas_call(
        functools.partial(kernel, n, nz, blk),
        out_shape=(
            jax.ShapeDtypeStruct((1, 64, FT), f32),
            jax.ShapeDtypeStruct((n, rows, 128), bf16),
        ),
        in_specs=[pl.BlockSpec(memory_space=pltpu.SMEM)] + [vm] * 5 + [hbm] * 14,
        out_specs=(vm, vm),
        scratch_shapes=scratch,
        compiler_params=pltpu.CompilerParams(
            collective_id=0, has_side_effects=True, vmem_limit_bytes=60 * 1024 * 1024
        ),
        name="dmd",
    )(
        sc, noise_field, time_real, time_fake, gain_real, gain_fake,
        hidden_states, gen_weight, embed_real, embed_fake, proj_real, proj_fake,
        out_real, out_fake,
        query_real, key_real, value_real, query_fake, key_fake, value_fake,
    )
    wg = wg.reshape(d // 128, 64, 128).transpose(1, 0, 2).reshape(64, d).astype(f32)
    return dmd, wg


def solution(mesh):
    in_specs = (
        P("batch", "tm", None), P(), P("batch", None, "tm"), P("batch"),
        P(), P("tm", None, None), P(None, "tm"), P(None, "tm"), P(None, "tm"),
        P("tm", None), P(None, "tm"), P(),
        P(), P("tm", None, None), P(None, "tm"), P(None, "tm"), P(None, "tm"),
        P("tm", None), P(None, "tm"), P(),
    )
    out_specs = (P("batch", None, "tm"), P())
    return jax.shard_map(
        per_device, mesh=mesh, in_specs=in_specs, out_specs=out_specs, check_vma=False
    )
```

time: 539 us -> 140 us (0.26); the launches traced: 533 us -> 140 us
  waiting for transfers between devices: 220 us -> 0 us
  matrix products: 142 us -> 0 us
  Pallas kernels: 0 us -> 131 us
  local copies, waits for them, and re-layouts: 45.3 us -> 4.4 us
  other arithmetic: 37.9 us -> 2.88 us
  loops' own time: 28.4 us -> 0 us
  starting transfers between devices: 22.4 us -> 0 us
  blocking collectives: 20.8 us -> 0 us
  between operations: 16.4 us -> 1.35 us
    psum x1 -> x0, waiting for transfers between devices: 146 us -> none  [per_device(): lax.psum(partial_grad / normalizer / grad_root, ('tm', 'batch'))]
    dot_general x64 -> x0, matrix products: 142 us -> none  [the longest x16 58.7 us: one_block(): jnp.einsum('qhd,khd->hqk', query_block, key_norm, preferred_element_type=...]
    pallas_call x0 -> x1, Pallas kernels: none -> 131 us  [per_device(): pl.pallas_call(functools.partial(kernel, n, nz, blk), out_shape=(jax.Shap...]
    all_gather x1 -> x0, waiting for transfers between devices: 58.9 us -> none  [rows_first(): filled = lax.all_gather(both, axis, axis=0, tiled=True)]
    reduce_sum x24 -> x0, other arithmetic: 28.5 us -> none  [the longest x16 20.4 us: one_block(): jnp.sum(exp_scores, axis=2, keepdims=True)]
    another operation x2 -> x0, loops' own time: 28.4 us -> none  [attend(): pieces = lax.map(one_block, starts)]
    all_to_all x1 -> x0, blocking collectives: 20.8 us -> none  [sum_at_owner(): tiles = lax.all_to_all(cut_along(shard, dim, size), axis, 0, 0, tiled=True)]
    all_to_all x3 -> x0, starting transfers between devices: 17.7 us -> none  [copy_for_each(): return lax.all_to_all(copies, axis, split_axis=0, concat_axis=0, tiled=True)]
  transfers between devices with their start and end apart: 6 -> 0, of which waited for: 4 -> 0; matrix products, arithmetic and copies ran while one was open for 6% -> 0% of each run, Pallas kernels for 0% -> 0%
where the time goes in v1:
time: 140 us
  Pallas kernels  131 us (94%)
  local copies, waits for them, and re-layouts  4.4 us (3%)
  other arithmetic  2.88 us (2%)
    pallas_call x1, Pallas kernels, per_device(): pl.pallas_call(functools.partial(kernel, n, nz, blk), out_shape=(jax.Shap...  131 us
    unnamed x5, local copies, waits for them, and re-layouts  4.4 us

profile of v1, /device:TPU:1, one launch (start us, length us, event | category | flops | bytes accessed | tf_op | source)
XLA Modules:
  0.0 139.7 jit_solution(16936485425104738697)
XLA Ops:
  1.3 0.1 compare_select_fusion.4
  1.4 0.6 pad_maximum_fusion.sc
  2.0 1.9 %copy.22.time_r = bf16[8,3,5120]{2,1,0:T(4,128)(2,1)} copy(bf16[8,3,5120]{2,0,1:T(8,128)(2,1)} %param.25) | data formatting | bytes 491520 | tf_op args[5]
  3.9 1.9 %copy.23.time_f = bf16[8,3,5120]{2,1,0:T(4,128)(2,1)} copy(bf16[8,3,5120]{2,0,1:T(8,128)(2,1)} %param.33) | data formatting | bytes 491520 | tf_op args[13]
  5.8 131.0 %dmd.1 = (f32[1,64,128]{2,1,0:T(8,128)}, bf16[32,80,128]{2,1,0:T(8,128)(2,1)}) custom-call(f32[16]{0:T(128)} %pad_maximum_fusion.sc, bf16[1,64,128]{2,1,0:T(8,128)(2,1)} %noise.1, bf16[8,3,5120]{2,1,0:T(4,128)(2,1)} %copy.22.time_r, bf16[8,3,5120]{2,1,0:T(4,128)(2,1)} %copy.23.time_f, f32[2,128]{1,0:T(2,128)} %gain_r.1, f32[2,128]{1,0:T(2,128)} %gain_f.1, ...), custom_call_target="tpu_custom_call" | custom-call | tf_op jit(solution)/shard_map/dmd/pallas_call | solution.py:529
  136.8 0.0 copy-start
  136.8 2.2 %copy_bitcast_fusion = f32[64,5120]{1,0:T(8,128)} fusion(bf16[40,64,128]{2,1,0:T(8,128)(2,1)} %bitcast.9), kind=kLoop, calls=%fused_computation | loop fusion | flops 327680 | bytes 1966080 | tf_op jit(solution)/shard_map/convert_element_type | solution.py:548
  139.1 0.0 copy-done
  139.1 0.6 copy.29
Async XLA Ops:
  136.8 2.2 %copy-start = (f32[1,64,128]{2,1,0:T(8,128)S(1)}, f32[1,64,128]{2,1,0:T(8,128)}, u32[]{:S(2)}) copy-start(f32[1,64,128]{2,1,0:T(8,128)} %get-tuple-element.10) | copy-start | bytes 98308

commit v2 on v1

v2 whole, which is shorter than its diff:
```python
import functools
import math

import jax
import jax.numpy as jnp
from jax import lax
from jax.experimental import pallas as pl
from jax.experimental.pallas import tpu as pltpu
from jax.sharding import PartitionSpec as P

HD = 128
FREQ = 256
FT = 128
MESH = pl.DeviceIdType.MESH

norm_floor = 0.05
gap_floor = 0.25
highest = lax.Precision.HIGHEST
f32 = jnp.float32
bf16 = jnp.bfloat16


def split2(a):
    hi = a.astype(bf16)
    lo = (a - hi.astype(f32)).astype(bf16)
    return hi, lo


def stack2(a):
    hi, lo = split2(a)
    return jnp.concatenate([hi, lo], axis=0)


def mm(a, b):
    return jnp.dot(a, b, preferred_element_type=f32)


def mm_t(a, b):
    return lax.dot_general(a, b, (((1,), (1,)), ((), ())), preferred_element_type=f32)


class Phase:
    def __init__(self):
        self.now = None

    def __call__(self, name):
        if self.now is not None:
            self.now.__exit__(None, None, None)
        self.now = None
        if name:
            self.now = jax.named_scope(name)
            self.now.__enter__()


def attend_block(block, blk, tokens, qt_ref, k_ref, v_ref, m_ref, o_ref, s_ref):
    q_at = pl.multiple_of(block * blk, blk)
    frames = blk // FT

    def score(net, k_at):
        return mm(k_ref[net, pl.ds(k_at, blk), :], qt_ref[net, :, pl.ds(q_at, blk)])

    for net in range(2):
        s_ref[net] = score(net, 0)
    for net in range(2):
        s = score(net, q_at)
        rows = []
        for r in range(frames):
            part = s[r * FT : (r + 1) * FT]
            if r:
                gone = jnp.full((FT, r * FT), -1e30, f32)
                part = jnp.concatenate([gone, part[:, r * FT :]], axis=1)
            rows.append(part)
        s = jnp.concatenate(rows, axis=0)
        top = jnp.max(s, axis=0, keepdims=True)
        p = jnp.exp2(s - top).astype(bf16)
        m_ref[net] = jnp.broadcast_to(top, (8, blk))
        o_ref[net] = mm(v_ref[net, :, pl.ds(q_at, blk)], p)

    def step(kb, _):
        k_at = pl.multiple_of(kb * blk, blk)
        next_at = pl.multiple_of(jnp.minimum(kb + 1, tokens // blk - 1) * blk, blk)
        for net in range(2):
            s = s_ref[net]
            old = m_ref[net, 0:1, :]
            top = jnp.maximum(old, jnp.max(s, axis=0, keepdims=True))
            p = jnp.exp2(s - top).astype(bf16)
            ahead = score(net, next_at)
            fade = jnp.exp2(old - top)
            o_ref[net] = o_ref[net] * fade + mm(v_ref[net, :, pl.ds(k_at, blk)], p)
            m_ref[net] = jnp.broadcast_to(top, (8, blk))
            s_ref[net] = ahead
        return 0

    lax.fori_loop(0, block, step, 0)


def block_at(s, me, per, blocks):
    home = me // per
    if blocks != 8:
        return lax.rem(home + 1 + s, blocks)
    dx = jnp.where(s < 2, 2, jnp.where(s < 6, 1 + 2 * lax.rem(s - 2, 2), 0))
    dy = jnp.where(s < 2, 1 - s, jnp.where(s < 4, 1, jnp.where(s < 6, 0, 7 - s)))
    x = lax.rem(home // 2 + dx, 4)
    y = lax.rem(home + dy, 2)
    return x * 2 + y


def kernel(
    n, nz, blk,
    sc, wave, noise, gain_r, gain_f,
    time_rh, time_fh, hidden_h, genw_h, emb_rh, emb_fh, proj_rh, proj_fh, out_rh, out_fh,
    wq_r, wk_r, wv_r, wq_f, wk_f, wv_f,
    dmd_ref, wg_ref,
    times, hid, genw, emb, proj, outw, wqk, wv,
    modbuf, modin, modfull, xg, xs, gen_s, mu_s, gmat, rmat,
    lhs, acc, lhs2, acc2, accv, rs_s, qraw, kraw, ktok, nbuf, nin, nfull,
    qt, kn, vt, m_s, o_s, s_s,
    tsend, trecv, gapbuf, wown, wgive, wtake, wsend, wrecv, zbuf,
    lsem, sem,
):
    me = lax.axis_index("tm")
    mz = lax.axis_index("batch")
    core = lax.rem(me, 2)
    chip = me // 2
    other = me + 1 - 2 * core
    chips = n // 2
    d = hid.shape[1]
    groups = d // 1024
    tokens = n * FT
    ph = Phase()
    loads = []

    def load(src, dst):
        c = pltpu.make_async_copy(src, dst, lsem.at[len(loads)])
        c.start()
        loads.append(c)
        return c

    ld_time = [load(time_rh, times.at[0]), load(time_fh, times.at[1])]
    ld_hid = load(hidden_h.at[0], hid)
    ld_gen = load(genw_h, genw)
    ld_emb = [load(emb_rh, emb.at[0]), load(emb_fh, emb.at[1])]
    ld_proj = [load(proj_rh, proj.at[0]), load(proj_fh, proj.at[1])]
    ld_qk = []
    for net, (a, b) in enumerate(((wq_r, wk_r), (wq_f, wk_f))):
        ld_qk.append(load(a, wqk.at[net, :, 0:HD]))
        ld_qk.append(load(b, wqk.at[net, :, HD : 2 * HD]))
    ld_v = [load(wv_r, wv.at[0]), load(wv_f, wv.at[1])]
    ld_out = [load(out_rh, outw.at[0]), load(out_fh, outw.at[1])]

    barrier = pltpu.get_barrier_semaphore()

    def greet(i, _):
        pl.semaphore_signal(
            barrier, inc=1, device_id={"tm": lax.rem(me + i, n)}, device_id_type=MESH
        )
        return 0

    lax.fori_loop(1, n, greet, 0)
    for i in range(1, nz):
        pl.semaphore_signal(
            barrier, inc=1, device_id={"batch": lax.rem(mz + i, nz)}, device_id_type=MESH
        )

    used = [0]

    class Lane:
        def __init__(self):
            self.send = sem.at[used[0]]
            self.recv = sem.at[used[0] + 1]
            used[0] += 2

        def to(self, src, dst, j, axis="tm"):
            return pltpu.make_async_remote_copy(
                src_ref=src, dst_ref=dst, send_sem=self.send, recv_sem=self.recv,
                device_id={axis: j}, device_id_type=MESH,
            )

        def all(self, src_of, dst):
            def body(i, _):
                j = lax.rem(me + i, n)
                self.to(src_of(j), dst, j).start()
                return 0

            lax.fori_loop(1, n, body, 0)

        def mates(self, src_of, dst):
            def body(i, _):
                j = lax.rem(chip + i, chips)
                self.to(src_of(j), dst, 2 * j + core).start()
                return 0

            lax.fori_loop(1, chips, body, 0)

        def wait(self, view):
            c = self.to(view, view, other)
            c.wait_recv()
            c.wait_send()

    mod_rs, mod_ag, xl, xf = Lane(), Lane(), Lane(), Lane()
    nrm_rs, nrm_ag, tl, gl = Lane(), Lane(), Lane(), Lane()
    w_pair, w_rs, w_z, w_ag, w_fw = Lane(), Lane(), Lane(), Lane(), Lane()

    ph("share")
    for p in range(6 * groups, n):
        modbuf[p] = jnp.zeros((8, 128), f32)
    for net in range(2):
        ld_time[net].wait()
        for c in range(3):
            for b in range(8 * groups):
                t = times[net, c, :, b * 128 : (b + 1) * 128].astype(f32)
                part = jnp.sum(t * wave[...], axis=0, keepdims=True)
                modbuf[(net * 3 + c) * groups + b // 8, b % 8 : b % 8 + 1, :] = part
    modin[me] = modbuf[me]

    ph("generate")
    ld_hid.wait()
    ld_gen.wait()
    generated = mm_t(genw[...], hid[...]).astype(bf16)
    gen_s[...] = generated
    xg[chip, core] = (sc[1] * generated.astype(f32) + sc[0] * noise[0].astype(f32)).astype(bf16)

    def weight_terms(net):
        ld_emb[net].wait()
        ld_proj[net].wait()

        def total(g, t):
            at = pl.multiple_of(g * 1024, 1024)
            return t + jnp.sum(emb[net, :, pl.ds(at, 1024)].astype(f32), axis=1, keepdims=True)

        mu = lax.fori_loop(0, groups, total, jnp.zeros((128, 1), f32)) / d
        mu_s[net] = jnp.broadcast_to(mu, (128, 128))

        def gram(g, t):
            at = pl.multiple_of(g * 1024, 1024)
            e = emb[net, :, pl.ds(at, 1024)]
            hi, lo = split2(e.astype(f32) - mu)
            both = jnp.concatenate([hi, lo], axis=0)
            return t[0] + mm_t(both, hi), t[1] + mm_t(proj[net, :, pl.ds(at, 1024)], e)

        gg, rr = lax.fori_loop(
            0, groups, gram, (jnp.zeros((256, 128), f32), jnp.zeros((64, 128), f32))
        )
        lh = gg[128:256]
        gmat[net] = stack2((gg[0:128] + lh + lh.T) / d)
        rmat[net] = stack2(rr)

    ph("weights0")
    weight_terms(0)
    ph("barrier")
    pl.semaphore_wait(barrier, n - 1 + nz - 1)
    mod_rs.all(lambda j: modbuf.at[j], modin.at[me])
    mine = xg.at[chip, core]
    xl.mates(lambda j: mine, mine)
    ph("weights1")
    weight_terms(1)

    ph("mod_rs")
    mod_rs.wait(modin.at[pl.ds(0, n - 1)])
    modfull[me] = jnp.sum(modin[...], axis=0)
    mod_ag.all(lambda j: modfull.at[me], modfull.at[me])

    ph("x_wait")
    xl.wait(xg.at[pl.ds(0, chips - 1), core])
    xf.to(xg.at[:, core], xg.at[:, core], other).start()
    xf.wait(xg.at[:, core])

    ph("place_var")

    def place(j, _):
        at = pl.multiple_of(j * FT, FT)
        xs[0:64, pl.ds(at, FT)] = xg[j // 2, lax.rem(j, 2)]
        return 0

    def place_late(j, _):
        at = pl.multiple_of(j * FT, FT)
        xs[64:128, pl.ds(at, FT)] = xg[(j - 1) // 2, lax.rem(j - 1, 2)]
        return 0

    xs[64:128, 0:FT] = jnp.zeros((64, FT), bf16)
    lax.fori_loop(0, n, place, 0)
    lax.fori_loop(1, n, place_late, 0)

    width = blk

    def variances(t, _):
        at = pl.multiple_of(t * width, width)
        x = xs[:, pl.ds(at, width)]
        for net in range(2):
            y = mm(gmat[net], x)
            var = jnp.sum((y[0:128] + y[128:256]) * x.astype(f32), axis=0, keepdims=True)
            rs = lax.rsqrt(jnp.maximum(var, 0.0) + norm_floor)
            rs_s[net, :, pl.ds(at, width)] = jnp.broadcast_to(rs, (8, width))
        return 0

    lax.fori_loop(0, tokens // width, variances, 0)
    for c in ld_qk:
        c.wait()
    ph("mod_ag_wait")
    mod_ag.wait(modfull.at[pl.ds(0, n - 1)])

    ph("qk_fold")
    row = lax.broadcasted_iota(jnp.int32, (16, 128), 0)
    acc[...] = jnp.zeros_like(acc)

    def fold(g, _):
        at = pl.multiple_of(g * 1024, 1024)
        for net in range(2):
            shift8 = modfull[(net * 3 + 0) * groups + g]
            scale8 = modfull[(net * 3 + 1) * groups + g]
            for r in range(8):
                col = pl.multiple_of(at + r * 128, 128)
                e = emb[net, :, pl.ds(col, 128)].astype(f32) - mu_s[net]
                lhs[net, 0:128, pl.ds(col, 128)] = (e * (1.0 + scale8[r : r + 1, :])).astype(bf16)
                sh, sl = split2(shift8[r : r + 1, :])
                tail = jnp.where(
                    row == 0, sh.astype(f32), jnp.where(row == 1, sl.astype(f32), 0.0)
                )
                lhs[net, 128:144, pl.ds(col, 128)] = tail.astype(bf16)
            acc[net] += mm(lhs[net, :, pl.ds(at, 1024)], wqk[net, pl.ds(at, 1024), :])
        return 0

    lax.fori_loop(0, groups, fold, 0)
    ph("qk_project")
    mats = []
    for net in range(2):
        off = acc[net, 128:129, :] + acc[net, 129:130, :]
        for which in range(2):
            cols = slice(which * HD, (which + 1) * HD)
            mat = acc[net, 0:128, cols].T.astype(bf16)
            mats.append((mat, jnp.broadcast_to(off[:, cols], (128, 128)).T[:, 0:1]))

    def project(t, _):
        at = pl.multiple_of(t * width, width)
        x = xs[:, pl.ds(at, width)]
        for net in range(2):
            rs = rs_s[net, 0:1, pl.ds(at, width)]
            for which, dst in enumerate((qraw, kraw)):
                mat, off_c = mats[net * 2 + which]
                y = mm(mat, x) * rs + off_c
                dst[net, :, pl.ds(at, width)] = y
                sq = jnp.sum(y * y, axis=0, keepdims=True)
                for r in range(width // FT):
                    nbuf[t * (width // FT) + r, net * 2 + which : net * 2 + which + 1, :] = sq[
                        :, r * FT : (r + 1) * FT
                    ]
        return 0

    lax.fori_loop(0, tokens // width, project, 0)

    ph("norm_send")
    nin[me] = nbuf[me]
    nrm_rs.all(lambda j: nbuf.at[j], nin.at[me])

    ph("v_fold")
    for c in ld_v + ld_out:
        c.wait()
    accv[...] = jnp.zeros_like(accv)
    acc2[...] = jnp.zeros_like(acc2)

    def fold_v(g, _):
        at = pl.multiple_of(g * 1024, 1024)
        for net in range(2):
            gate8 = modfull[(net * 3 + 2) * groups + g]
            for r in range(8):
                col = pl.multiple_of(at + r * 128, 128)
                gated = proj[net, :, pl.ds(col, 128)].astype(f32) * gate8[r : r + 1, :]
                hi, lo = split2(gated)
                lhs2[net, 0:64, r * 128 : (r + 1) * 128] = hi
                lhs2[net, 64:128, r * 128 : (r + 1) * 128] = lo
            accv[net] += mm(lhs[net, :, pl.ds(at, 1024)], wv[net, pl.ds(at, 1024), :])
            acc2[net] += mm_t(lhs2[net], outw[net, :, pl.ds(at, 1024)])
        return 0

    lax.fori_loop(0, groups, fold_v, 0)

    ph("norm_rs_wait")
    nrm_rs.wait(nin.at[pl.ds(0, n - 1)])
    nfull[me] = lax.rsqrt(jnp.sum(nin[...], axis=0) / float(n * HD) + norm_floor)
    nrm_ag.all(lambda j: nfull.at[me], nfull.at[me])

    ph("values")
    vmats = []
    for net in range(2):
        a = accv[net, 0:128, :]
        off = accv[net, 128:129, :] + accv[net, 129:130, :]
        out_t = acc2[net, 0:64, :] + acc2[net, 64:128, :]
        b_mat = stack2(
            lax.dot_general(
                out_t, a, (((1,), (1,)), ((), ())), precision=highest, preferred_element_type=f32
            )
        )
        vmats.append((b_mat, jnp.sum(out_t * off, axis=1, keepdims=True)))
    ones = jnp.where(lax.broadcasted_iota(jnp.int32, (16, width), 0) == 0, 1.0, 0.0)

    def values(t, _):
        at = pl.multiple_of(t * width, width)
        x = xs[:, pl.ds(at, width)]
        for net in range(2):
            y = mm(vmats[net][0], x)
            y = (y[0:64] + y[64:128]) * rs_s[net, 0:1, pl.ds(at, width)] + vmats[net][1]
            vt[net, 0:64, pl.ds(at, width)] = y.astype(bf16)
            vt[net, 64:80, pl.ds(at, width)] = ones.astype(bf16)
        return 0

    lax.fori_loop(0, tokens // width, values, 0)
    ph("turn")
    gains = []
    for gain in (gain_r, gain_f):
        both = gain[0:1, :] * gain[1:2, :] * (math.log2(math.e) / math.sqrt(HD))
        gains.append(jnp.broadcast_to(both, (128, 128)).T)

    def turn(j, _):
        at = pl.multiple_of(j * FT, FT)
        for net in range(2):
            ktok[net, pl.ds(at, FT), :] = kraw[net, :, pl.ds(at, FT)].T
            qraw[net, :, pl.ds(at, FT)] = qraw[net, :, pl.ds(at, FT)] * gains[net]
        return 0

    lax.fori_loop(0, n, turn, 0)
    ph("norm_ag_wait")
    nrm_ag.wait(nfull.at[pl.ds(0, n - 1)])

    ph("normalise")

    def normalise(j, _):
        at = pl.multiple_of(j * FT, FT)
        scales = nfull[j]
        tall = jnp.concatenate([scales] * 16, axis=0).T
        for net in range(2):
            sq = scales[net * 2 : net * 2 + 1, :]
            sk = tall[:, net * 2 + 1 : net * 2 + 2]
            qt[net, :, pl.ds(at, FT)] = (qraw[net, :, pl.ds(at, FT)] * sq).astype(bf16)
            kn[net, pl.ds(at, FT), :] = (ktok[net, pl.ds(at, FT), :] * sk).astype(bf16)
        return 0

    lax.fori_loop(0, n, normalise, 0)

    ph("attend")
    blocks = tokens // blk
    per = blk // FT

    def one_block(s, _):
        block = block_at(s, me, per, blocks)
        attend_block(block, blk, tokens, qt, kn, vt, m_s, o_s, s_s)
        for net in range(2):
            o = o_s[net]
            y = (o[0:64] / o[64:65]).astype(bf16)
            for r in range(per):
                tsend[block * per + r, net * 64 : (net + 1) * 64, :] = y[:, r * FT : (r + 1) * FT]
        for r in range(per):
            f = block * per + r

            @pl.when(f != me)
            def _():
                tl.to(tsend.at[f], trecv.at[me], f).start()

        return 0

    lax.fori_loop(0, blocks, one_block, 0)
    ph("t_wait")
    trecv[me] = tsend[me]
    tl.wait(trecv.at[pl.ds(0, n - 1)])

    ph("finish")

    def add_up(s, t):
        return t + trecv[s].astype(f32)

    vel = lax.fori_loop(0, n, add_up, jnp.zeros((128, FT), f32))
    x_own = xs[:, pl.ds(pl.multiple_of(me * FT, FT), FT)]
    base_r = mm(rmat[0], x_own)
    base_f = mm(rmat[1], x_own)
    vel_r = vel[0:64] + base_r[0:64] + base_r[64:128]
    vel_f = vel[64:128] + base_f[0:64] + base_f[64:128]
    noisy = x_own[0:64].astype(f32)
    pred_r = noisy - sc[0] * vel_r
    pred_f = noisy - sc[0] * vel_f
    gap = jnp.abs(gen_s[...].astype(f32) - pred_r)
    gsum = gap[0:8]
    for r in range(1, 8):
        gsum = gsum + gap[r * 8 : (r + 1) * 8]
    gapbuf[me] = gsum
    gl.all(lambda j: gapbuf.at[me], gapbuf.at[me])
    diff = pred_f - pred_r
    dmd_ref[0] = diff
    diff_b = diff.astype(bf16)

    ph("wg_mm")
    half = d // 2
    stride = 512

    def wg_part(h, dst):
        def body(g, _):
            at = pl.multiple_of(h * half + g * stride, stride)
            y = mm(diff_b, hid[:, pl.ds(at, stride)])
            for r in range(stride // 128):
                to = pl.multiple_of((g * (stride // 128) + r) * 64, 64)
                dst[pl.ds(to, 64), :] = y[:, r * 128 : (r + 1) * 128].astype(dst.dtype)
            return 0

        lax.fori_loop(0, half // stride, body, 0)

    wg_part(1 - core, wgive)
    w_pair.to(wgive, wtake, other).start()
    wg_part(core, wown)
    ph("w_pair")
    w_pair.wait(wtake)
    rows = wrecv.shape[1]

    def pair_sum(j, _):
        at = pl.ds(pl.multiple_of(j * rows, 16), rows)
        wsend[j] = (wown[at, :] + wtake[at, :].astype(f32)).astype(bf16)
        return 0

    lax.fori_loop(0, chips, pair_sum, 0)
    w_rs.mates(lambda j: wsend.at[j], wrecv.at[chip])
    wrecv[chip] = wsend[chip]
    ph("gap_wait")
    gl.wait(gapbuf.at[pl.ds(0, n - 1)])
    gap_all = jnp.sum(jnp.sum(gapbuf[...], axis=0), keepdims=True)
    inv = 1.0 / jnp.maximum(gap_all / (64.0 * tokens), gap_floor)
    dmd_ref[0] = dmd_ref[0] * inv
    ph("w_wait")
    w_rs.wait(wrecv.at[pl.ds(0, chips - 1)])

    def add_w(s, t):
        return t + wrecv[s].astype(f32)

    wsum = lax.fori_loop(0, chips, add_w, jnp.zeros((rows, 128), f32))
    zbuf[mz] = (wsum * (inv / math.sqrt(nz * tokens))).astype(bf16)
    ph("w_z")
    for i in range(1, nz):
        w_z.to(zbuf.at[mz], zbuf.at[mz], lax.rem(mz + i, nz), "batch").start()
    zview = zbuf.at[pl.ds(0, nz - 1)]
    zwait = w_z.to(zview, zview, lax.rem(mz + 1, nz), "batch")
    zwait.wait_recv()
    zwait.wait_send()
    whole = zbuf[0].astype(f32)
    for z in range(1, nz):
        whole = whole + zbuf[z].astype(f32)
    ph("w_ag")
    wg_ref[core, chip] = whole.astype(bf16)
    part = wg_ref.at[core, chip]
    w_ag.mates(lambda j: part, part)
    w_ag.wait(wg_ref.at[core, pl.ds(0, chips - 1)])
    ph("w_forward")
    w_fw.to(wg_ref.at[core], wg_ref.at[core], other).start()
    w_fw.wait(wg_ref.at[core])
    ph(None)


def per_device(
    hidden_states, gen_weight, noise_field, timesteps,
    embed_real, time_real, query_real, key_real, value_real, out_real, gain_real, proj_real,
    embed_fake, time_fake, query_fake, key_fake, value_fake, out_fake, gain_fake, proj_fake,
):
    n = lax.axis_size("tm")
    nz = lax.axis_size("batch")
    d = hidden_states.shape[2]
    tokens = n * FT
    blk = 512
    rows = 64 * d // 128 // n
    chips = n // 2
    fr = time_real.shape[0]
    step = timesteps[0].astype(f32)
    raw = step / 1000.0
    sigma = 5.0 * raw / (1.0 + 4.0 * raw)
    half = FREQ // 2
    at = lax.axis_index("tm") * fr + jnp.arange(fr, dtype=jnp.int32)
    freq = jnp.exp(-math.log(10000.0) * (at % half).astype(f32) / half)
    wave = jnp.where(at < half, jnp.cos(step * freq), jnp.sin(step * freq))
    wave = wave.astype(bf16).astype(f32)
    wave = jnp.broadcast_to(wave[:, None], (fr, 128))
    slot = jnp.arange(8)
    sc = jnp.where(slot == 0, sigma, jnp.where(slot == 1, 1.0 - sigma, 0.0))

    vm = pl.BlockSpec(memory_space=pltpu.VMEM)
    hbm = pl.BlockSpec(memory_space=pl.ANY)
    sems = pltpu.SemaphoreType.DMA
    scratch = [
        pltpu.VMEM((2, 3, fr, d), bf16),
        pltpu.VMEM((FT, d), bf16),
        pltpu.VMEM((64, d), bf16),
        pltpu.VMEM((2, 128, d), bf16),
        pltpu.VMEM((2, 64, d), bf16),
        pltpu.VMEM((2, 128, d), bf16),
        pltpu.VMEM((2, d, 256), bf16),
        pltpu.VMEM((2, d, 128), bf16),
        pltpu.VMEM((n, 8, 128), f32),
        pltpu.VMEM((n, 8, 128), f32),
        pltpu.VMEM((n, 8, 128), f32),
        pltpu.VMEM((chips, 2, 64, 128), bf16),
        pltpu.VMEM((128, tokens), bf16),
        pltpu.VMEM((64, 128), bf16),
        pltpu.VMEM((2, 128, 128), f32),
        pltpu.VMEM((2, 256, 128), bf16),
        pltpu.VMEM((2, 128, 128), bf16),
        pltpu.VMEM((2, 144, d), bf16),
        pltpu.VMEM((2, 144, 256), f32),
        pltpu.VMEM((2, 128, 1024), bf16),
        pltpu.VMEM((2, 128, 128), f32),
        pltpu.VMEM((2, 144, 128), f32),
        pltpu.VMEM((2, 8, tokens), f32),
        pltpu.VMEM((2, 128, tokens), f32),
        pltpu.VMEM((2, 128, tokens), f32),
        pltpu.VMEM((2, tokens, 128), f32),
        pltpu.VMEM((n, 8, 128), f32),
        pltpu.VMEM((n, 8, 128), f32),
        pltpu.VMEM((n, 8, 128), f32),
        pltpu.VMEM((2, 128, tokens), bf16),
        pltpu.VMEM((2, tokens, 128), bf16),
        pltpu.VMEM((2, 80, tokens), bf16),
        pltpu.VMEM((2, 8, blk), f32),
        pltpu.VMEM((2, 80, blk), f32),
        pltpu.VMEM((2, blk, blk), f32),
        pltpu.VMEM((n, 128, 128), bf16),
        pltpu.VMEM((n, 128, 128), bf16),
        pltpu.VMEM((n, 8, 128), f32),
        pltpu.VMEM((rows * chips, 128), f32),
        pltpu.VMEM((rows * chips, 128), bf16),
        pltpu.VMEM((rows * chips, 128), bf16),
        pltpu.VMEM((chips, rows, 128), bf16),
        pltpu.VMEM((chips, rows, 128), bf16),
        pltpu.VMEM((nz, rows, 128), bf16),
        sems((16,)),
        sems((26,)),
    ]
    dmd, wg = pl.pallas_call(
        functools.partial(kernel, n, nz, blk),
        out_shape=(
            jax.ShapeDtypeStruct((1, 64, FT), f32),
            jax.ShapeDtypeStruct((2, chips, rows, 128), bf16),
        ),
        in_specs=[pl.BlockSpec(memory_space=pltpu.SMEM)] + [vm] * 4 + [hbm] * 16,
        out_specs=(vm, vm),
        scratch_shapes=scratch,
        compiler_params=pltpu.CompilerParams(
            collective_id=0, has_side_effects=True, vmem_limit_bytes=62 * 1024 * 1024
        ),
        name="dmd",
    )(
        sc, wave, noise_field, gain_real, gain_fake,
        time_real.transpose(1, 0, 2), time_fake.transpose(1, 0, 2),
        hidden_states, gen_weight, embed_real, embed_fake, proj_real, proj_fake,
        out_real, out_fake,
        query_real, key_real, value_real, query_fake, key_fake, value_fake,
    )
    wg = wg.reshape(d // 128, 64, 128).transpose(1, 0, 2).reshape(64, d).astype(f32)
    return dmd, wg


def solution(mesh):
    in_specs = (
        P("batch", "tm", None), P(), P("batch", None, "tm"), P("batch"),
        P(), P("tm", None, None), P(None, "tm"), P(None, "tm"), P(None, "tm"),
        P("tm", None), P(None, "tm"), P(),
        P(), P("tm", None, None), P(None, "tm"), P(None, "tm"), P(None, "tm"),
        P("tm", None), P(None, "tm"), P(),
    )
    out_specs = (P("batch", None, "tm"), P())
    return jax.shard_map(
        per_device, mesh=mesh, in_specs=in_specs, out_specs=out_specs, check_vma=False
    )
```

time: 140 us -> 108 us (0.77)
  Pallas kernels: 131 us -> 102 us
  local copies, waits for them, and re-layouts: 4.4 us -> 1.29 us
    pallas_call x1, Pallas kernels: 131 us -> 102 us  [per_device(): pl.pallas_call(functools.partial(kernel, n, nz, blk), out_shape=(jax.Shap...]
    unnamed x5 -> x3, local copies, waits for them, and re-layouts: 4.4 us -> 0.62 us
where the time goes in v2:
time: 108 us
  Pallas kernels  102 us (94%)
  other arithmetic  2.8 us (3%)
  between operations  1.35 us (1%)
  local copies, waits for them, and re-layouts  1.29 us (1%)
    pallas_call x1, Pallas kernels, per_device(): pl.pallas_call(functools.partial(kernel, n, nz, blk), out_shape=(jax.Shap...  102 us
    convert_element_type x1, other arithmetic, per_device(): wg.reshape(d // 128, 64, 128).transpose(1, 0, 2).reshape(64, d).astype(f32)  2.23 us

profile of v2, /device:TPU:1, one launch (start us, length us, event | category | flops | bytes accessed | tf_op | source)
XLA Modules:
  0.0 107.5 jit_solution(16232359577076785839)
XLA Ops:
  1.3 0.5 compare_select_fusion.4.sc
  1.8 0.1 fusion.1
  1.9 0.7 broadcast_in_dim.21.wave
  2.6 102.1 %dmd.1 = (f32[1,64,128]{2,1,0:T(8,128)}, bf16[2,16,80,128]{3,2,1,0:T(8,128)(2,1)}) custom-call(f32[8]{0:T(128)} %compare_select_fusion.4.sc, f32[8,128]{1,0:T(8,128)} %broadcast_in_dim.21.wave, bf16[1,64,128]{2,1,0:T(8,128)(2,1)} %noise.1, f32[2,128]{1,0:T(2,128)} %gain_r.1, f32[2,128]{1,0:T(2,128)} %gain_f.1, bf16[3,8,5120]{2,1,0:T(8,128)(2,1)} %bitcast.12, ...), custom_call_target="tpu_custom_call" | custom-call | tf_op jit(solution)/shard_map/dmd/pallas_call | solution.py:629
  104.7 0.0 copy-start
  104.7 2.2 %copy_bitcast_fusion = f32[64,5120]{1,0:T(8,128)} fusion(bf16[40,64,128]{2,1,0:T(8,128)(2,1)} %bitcast.11), kind=kLoop, calls=%fused_computation | loop fusion | flops 327680 | bytes 1966080 | tf_op jit(solution)/shard_map/convert_element_type | solution.py:649
  106.9 0.0 copy-done
  106.9 0.6 copy.27
Async XLA Ops:
  104.7 2.2 %copy-start = (f32[1,64,128]{2,1,0:T(8,128)S(1)}, f32[1,64,128]{2,1,0:T(8,128)}, u32[]{:S(2)}) copy-start(f32[1,64,128]{2,1,0:T(8,128)} %get-tuple-element.8) | copy-start | bytes 98308

commit v3 on v2

--- a/solution.py
+++ b/solution.py
@@ -11,6 +11,7 @@
 HD = 128
 FREQ = 256
 FT = 128
+GS = 8
 MESH = pl.DeviceIdType.MESH
 
 norm_floor = 0.05
@@ -113,9 +114,9 @@
     dmd_ref, wg_ref,
     times, hid, genw, emb, proj, outw, wqk, wv,
     modbuf, modin, modfull, xg, xs, gen_s, mu_s, gmat, rmat,
-    lhs, acc, lhs2, acc2, accv, rs_s, qraw, kraw, ktok, nbuf, nin, nfull,
+    lhs, acc, lhs2, acc2, accv, rs_s, qraw, kraw, nbuf, nin, nfull,
     qt, kn, vt, m_s, o_s, s_s,
-    tsend, trecv, gapbuf, wown, wgive, wtake, wsend, wrecv, zbuf,
+    tsend, trecv, gapbuf, hcol, dcat, wsend, wrecv, zbuf,
     lsem, sem,
 ):
     me = lax.axis_index("tm")
@@ -199,7 +200,11 @@
 
     mod_rs, mod_ag, xl, xf = Lane(), Lane(), Lane(), Lane()
     nrm_rs, nrm_ag, tl, gl = Lane(), Lane(), Lane(), Lane()
-    w_pair, w_rs, w_z, w_ag, w_fw = Lane(), Lane(), Lane(), Lane(), Lane()
+    hl, dl, w_rs, w_z, w_ag, w_fw = Lane(), Lane(), Lane(), Lane(), Lane(), Lane()
+    member = lax.rem(me, GS)
+    home = me - member
+    gx = n // GS
+    myx = me // GS
 
     ph("share")
     for p in range(6 * groups, n):
@@ -213,47 +218,40 @@
                 modbuf[(net * 3 + c) * groups + b // 8, b % 8 : b % 8 + 1, :] = part
     modin[me] = modbuf[me]
 
+    ph("barrier")
+    pl.semaphore_wait(barrier, n - 1 + nz - 1)
+    mod_rs.all(lambda j: modbuf.at[j], modin.at[me])
+
     ph("generate")
     ld_hid.wait()
     ld_gen.wait()
     generated = mm_t(genw[...], hid[...]).astype(bf16)
     gen_s[...] = generated
     xg[chip, core] = (sc[1] * generated.astype(f32) + sc[0] * noise[0].astype(f32)).astype(bf16)
-
-    def weight_terms(net):
+    mine = xg.at[chip, core]
+    xl.mates(lambda j: mine, mine)
+
+    ph("weights")
+    ones_k = jnp.ones((1024, 128), bf16)
+    for net in range(2):
         ld_emb[net].wait()
         ld_proj[net].wait()
-
-        def total(g, t):
-            at = pl.multiple_of(g * 1024, 1024)
-            return t + jnp.sum(emb[net, :, pl.ds(at, 1024)].astype(f32), axis=1, keepdims=True)
-
-        mu = lax.fori_loop(0, groups, total, jnp.zeros((128, 1), f32)) / d
-        mu_s[net] = jnp.broadcast_to(mu, (128, 128))
 
         def gram(g, t):
             at = pl.multiple_of(g * 1024, 1024)
             e = emb[net, :, pl.ds(at, 1024)]
-            hi, lo = split2(e.astype(f32) - mu)
-            both = jnp.concatenate([hi, lo], axis=0)
-            return t[0] + mm_t(both, hi), t[1] + mm_t(proj[net, :, pl.ds(at, 1024)], e)
-
-        gg, rr = lax.fori_loop(
-            0, groups, gram, (jnp.zeros((256, 128), f32), jnp.zeros((64, 128), f32))
-        )
-        lh = gg[128:256]
-        gmat[net] = stack2((gg[0:128] + lh + lh.T) / d)
+            return (
+                t[0] + mm_t(e, e),
+                t[1] + mm(e, ones_k),
+                t[2] + mm_t(proj[net, :, pl.ds(at, 1024)], e),
+            )
+
+        zero = jnp.zeros((128, 128), f32)
+        ee, mu, rr = lax.fori_loop(0, groups, gram, (zero, zero, jnp.zeros((64, 128), f32)))
+        mu = mu / d
+        mu_s[net] = mu
+        gmat[net] = stack2(ee / d - mu * mu.T)
         rmat[net] = stack2(rr)
-
-    ph("weights0")
-    weight_terms(0)
-    ph("barrier")
-    pl.semaphore_wait(barrier, n - 1 + nz - 1)
-    mod_rs.all(lambda j: modbuf.at[j], modin.at[me])
-    mine = xg.at[chip, core]
-    xl.mates(lambda j: mine, mine)
-    ph("weights1")
-    weight_terms(1)
 
     ph("mod_rs")
     mod_rs.wait(modin.at[pl.ds(0, n - 1)])
@@ -273,13 +271,13 @@
         return 0
 
     def place_late(j, _):
-        at = pl.multiple_of(j * FT, FT)
-        xs[64:128, pl.ds(at, FT)] = xg[(j - 1) // 2, lax.rem(j - 1, 2)]
+        at = pl.multiple_of(j * FT + FT, FT)
+        xs[64:128, pl.ds(at, FT)] = xg[j // 2, lax.rem(j, 2)]
         return 0
 
     xs[64:128, 0:FT] = jnp.zeros((64, FT), bf16)
-    lax.fori_loop(0, n, place, 0)
-    lax.fori_loop(1, n, place_late, 0)
+    lax.fori_loop(0, n, place, 0, unroll=8)
+    lax.fori_loop(0, n - 1, place_late, 0, unroll=8)
 
     width = blk
 
@@ -293,7 +291,7 @@
             rs_s[net, :, pl.ds(at, width)] = jnp.broadcast_to(rs, (8, width))
         return 0
 
-    lax.fori_loop(0, tokens // width, variances, 0)
+    lax.fori_loop(0, tokens // width, variances, 0, unroll=2)
     for c in ld_qk:
         c.wait()
     ph("mod_ag_wait")
@@ -346,7 +344,7 @@
                     ]
         return 0
 
-    lax.fori_loop(0, tokens // width, project, 0)
+    lax.fori_loop(0, tokens // width, project, 0, unroll=2)
 
     ph("norm_send")
     nin[me] = nbuf[me]
@@ -403,38 +401,50 @@
             vt[net, 64:80, pl.ds(at, width)] = ones.astype(bf16)
         return 0
 
-    lax.fori_loop(0, tokens // width, values, 0)
-    ph("turn")
+    lax.fori_loop(0, tokens // width, values, 0, unroll=2)
     gains = []
     for gain in (gain_r, gain_f):
         both = gain[0:1, :] * gain[1:2, :] * (math.log2(math.e) / math.sqrt(HD))
         gains.append(jnp.broadcast_to(both, (128, 128)).T)
-
-    def turn(j, _):
-        at = pl.multiple_of(j * FT, FT)
-        for net in range(2):
-            ktok[net, pl.ds(at, FT), :] = kraw[net, :, pl.ds(at, FT)].T
-            qraw[net, :, pl.ds(at, FT)] = qraw[net, :, pl.ds(at, FT)] * gains[net]
-        return 0
-
-    lax.fori_loop(0, n, turn, 0)
+    same = lax.broadcasted_iota(jnp.int32, (256, 256), 0) == lax.broadcasted_iota(
+        jnp.int32, (256, 256), 1
+    )
+    eye = jnp.where(same, 1.0, 0.0).astype(bf16)
     ph("norm_ag_wait")
     nrm_ag.wait(nfull.at[pl.ds(0, n - 1)])
 
     ph("normalise")
 
-    def normalise(j, _):
-        at = pl.multiple_of(j * FT, FT)
-        scales = nfull[j]
-        tall = jnp.concatenate([scales] * 16, axis=0).T
-        for net in range(2):
-            sq = scales[net * 2 : net * 2 + 1, :]
-            sk = tall[:, net * 2 + 1 : net * 2 + 2]
-            qt[net, :, pl.ds(at, FT)] = (qraw[net, :, pl.ds(at, FT)] * sq).astype(bf16)
-            kn[net, pl.ds(at, FT), :] = (ktok[net, pl.ds(at, FT), :] * sk).astype(bf16)
-        return 0
-
-    lax.fori_loop(0, n, normalise, 0)
+    def normalise(t, _):
+        at = pl.multiple_of(t * 256, 256)
+        k_rows = []
+        for net in range(2):
+            k_cols = []
+            for half in range(2):
+                scales = nfull[t * 2 + half]
+                to = pl.ds(pl.multiple_of(at + half * FT, FT), FT)
+                sq = scales[net * 2 : net * 2 + 1, :]
+                sk = scales[net * 2 + 1 : net * 2 + 2, :]
+                qt[net, :, to] = (qraw[net, :, to] * sq * gains[net]).astype(bf16)
+                k_cols.append((kraw[net, :, to] * sk).astype(bf16))
+            k_rows.append(jnp.concatenate(k_cols, axis=1))
+        turned = mm_t(eye, jnp.concatenate(k_rows, axis=0)).astype(bf16)
+        for net in range(2):
+            kn[net, pl.ds(at, 256), :] = turned[:, net * HD : (net + 1) * HD]
+        return 0
+
+    lax.fori_loop(0, tokens // 256, normalise, 0, unroll=2)
+
+    def share_cols(i, _):
+        j = lax.rem(member + i, GS)
+        src = hid.at[:, pl.ds(pl.multiple_of(j * hcol.shape[1], 128), hcol.shape[1])]
+        hl.to(src, hcol.at[pl.ds(pl.multiple_of(member * FT, FT), FT), :], home + j).start()
+        return 0
+
+    lax.fori_loop(1, GS, share_cols, 0)
+    hcol[pl.ds(pl.multiple_of(member * FT, FT), FT), :] = hid[
+        :, pl.ds(pl.multiple_of(member * hcol.shape[1], 128), hcol.shape[1])
+    ]
 
     ph("attend")
     blocks = tokens // blk
@@ -459,21 +469,21 @@
 
     lax.fori_loop(0, blocks, one_block, 0)
     ph("t_wait")
-    trecv[me] = tsend[me]
-    tl.wait(trecv.at[pl.ds(0, n - 1)])
-
-    ph("finish")
-
-    def add_up(s, t):
-        return t + trecv[s].astype(f32)
-
-    vel = lax.fori_loop(0, n, add_up, jnp.zeros((128, FT), f32))
     x_own = xs[:, pl.ds(pl.multiple_of(me * FT, FT), FT)]
     base_r = mm(rmat[0], x_own)
     base_f = mm(rmat[1], x_own)
+    noisy = x_own[0:64].astype(f32)
+    trecv[me] = tsend[me]
+    tl.wait(trecv.at[pl.ds(0, n - 1)])
+
+    ph("finish")
+
+    def add_up(s, t):
+        return t + trecv[s].astype(f32)
+
+    vel = lax.fori_loop(0, n, add_up, jnp.zeros((128, FT), f32), unroll=8)
     vel_r = vel[0:64] + base_r[0:64] + base_r[64:128]
     vel_f = vel[64:128] + base_f[0:64] + base_f[64:128]
-    noisy = x_own[0:64].astype(f32)
     pred_r = noisy - sc[0] * vel_r
     pred_f = noisy - sc[0] * vel_f
     gap = jnp.abs(gen_s[...].astype(f32) - pred_r)
@@ -481,72 +491,71 @@
     for r in range(1, 8):
         gsum = gsum + gap[r * 8 : (r + 1) * 8]
     gapbuf[me] = gsum
+    diff = pred_f - pred_r
+    own = dcat.at[:, pl.ds(pl.multiple_of(member * FT, FT), FT)]
+    own[...] = diff.astype(bf16)
+
+    def share_diff(i, _):
+        dl.to(own, own, home + lax.rem(member + i, GS)).start()
+        return 0
+
+    lax.fori_loop(1, GS, share_diff, 0)
     gl.all(lambda j: gapbuf.at[me], gapbuf.at[me])
-    diff = pred_f - pred_r
     dmd_ref[0] = diff
-    diff_b = diff.astype(bf16)
-
+    ph("h_wait")
+    hl.wait(hcol.at[pl.ds(0, (GS - 1) * FT), :])
+    ph("d_wait")
+    dl.wait(dcat.at[:, pl.ds(0, (GS - 1) * FT)])
     ph("wg_mm")
-    half = d // 2
-    stride = 512
-
-    def wg_part(h, dst):
-        def body(g, _):
-            at = pl.multiple_of(h * half + g * stride, stride)
-            y = mm(diff_b, hid[:, pl.ds(at, stride)])
-            for r in range(stride // 128):
-                to = pl.multiple_of((g * (stride // 128) + r) * 64, 64)
-                dst[pl.ds(to, 64), :] = y[:, r * 128 : (r + 1) * 128].astype(dst.dtype)
-            return 0
-
-        lax.fori_loop(0, half // stride, body, 0)
-
-    wg_part(1 - core, wgive)
-    w_pair.to(wgive, wtake, other).start()
-    wg_part(core, wown)
-    ph("w_pair")
-    w_pair.wait(wtake)
+    wsend[...] = mm(dcat[...], hcol[...]).astype(bf16)
     rows = wrecv.shape[1]
 
-    def pair_sum(j, _):
-        at = pl.ds(pl.multiple_of(j * rows, 16), rows)
-        wsend[j] = (wown[at, :] + wtake[at, :].astype(f32)).astype(bf16)
-        return 0
-
-    lax.fori_loop(0, chips, pair_sum, 0)
-    w_rs.mates(lambda j: wsend.at[j], wrecv.at[chip])
-    wrecv[chip] = wsend[chip]
+    def x_rows(x):
+        return pl.ds(pl.multiple_of(x * rows, 16), rows)
+
+    for i in range(1, gx):
+        x = lax.rem(myx + i, gx)
+        w_rs.to(wsend.at[x_rows(x), :], wrecv.at[myx], x * GS + member).start()
+    wrecv[myx] = wsend[x_rows(myx), :]
     ph("gap_wait")
     gl.wait(gapbuf.at[pl.ds(0, n - 1)])
     gap_all = jnp.sum(jnp.sum(gapbuf[...], axis=0), keepdims=True)
     inv = 1.0 / jnp.maximum(gap_all / (64.0 * tokens), gap_floor)
     dmd_ref[0] = dmd_ref[0] * inv
     ph("w_wait")
-    w_rs.wait(wrecv.at[pl.ds(0, chips - 1)])
-
-    def add_w(s, t):
-        return t + wrecv[s].astype(f32)
-
-    wsum = lax.fori_loop(0, chips, add_w, jnp.zeros((rows, 128), f32))
+    if gx > 1:
+        w_rs.wait(wrecv.at[pl.ds(0, gx - 1)])
+    wsum = wrecv[0].astype(f32)
+    for x in range(1, gx):
+        wsum = wsum + wrecv[x].astype(f32)
     zbuf[mz] = (wsum * (inv / math.sqrt(nz * tokens))).astype(bf16)
     ph("w_z")
     for i in range(1, nz):
         w_z.to(zbuf.at[mz], zbuf.at[mz], lax.rem(mz + i, nz), "batch").start()
-    zview = zbuf.at[pl.ds(0, nz - 1)]
-    zwait = w_z.to(zview, zview, lax.rem(mz + 1, nz), "batch")
-    zwait.wait_recv()
-    zwait.wait_send()
+    if nz > 1:
+        zview = zbuf.at[pl.ds(0, nz - 1)]
+        zwait = w_z.to(zview, zview, lax.rem(mz + 1, nz), "batch")
+        zwait.wait_recv()
+        zwait.wait_send()
     whole = zbuf[0].astype(f32)
     for z in range(1, nz):
         whole = whole + zbuf[z].astype(f32)
     ph("w_ag")
-    wg_ref[core, chip] = whole.astype(bf16)
-    part = wg_ref.at[core, chip]
+    cols = wrecv.shape[2]
+
+    def col(g):
+        return pl.ds(pl.multiple_of(g * cols, 128), cols)
+
+    part = wg_ref.at[x_rows(myx), col(member)]
+    part[...] = whole.astype(bf16)
     w_ag.mates(lambda j: part, part)
-    w_ag.wait(wg_ref.at[core, pl.ds(0, chips - 1)])
+    fold_by = next(k for k in range(1, chips) if (chips - 1) % k == 0 and (chips - 1) // k <= GS)
+    w_ag.wait(wg_ref.at[pl.ds(0, fold_by * rows), pl.ds(0, (chips - 1) // fold_by * cols)])
     ph("w_forward")
-    w_fw.to(wg_ref.at[core], wg_ref.at[core], other).start()
-    w_fw.wait(wg_ref.at[core])
+    for y in range(GS // 2):
+        view = wg_ref.at[:, col(2 * y + core)]
+        w_fw.to(view, view, other).start()
+    w_fw.wait(wg_ref.at[:, pl.ds(0, d // 2)])
     ph(None)
 
 
@@ -560,8 +569,10 @@
     d = hidden_states.shape[2]
     tokens = n * FT
     blk = 512
-    rows = 64 * d // 128 // n
     chips = n // 2
+    gx = n // GS
+    rows = 64 // gx
+    cols = d // GS
     fr = time_real.shape[0]
     step = timesteps[0].astype(f32)
     raw = step / 1000.0
@@ -604,7 +615,6 @@
         pltpu.VMEM((2, 8, tokens), f32),
         pltpu.VMEM((2, 128, tokens), f32),
         pltpu.VMEM((2, 128, tokens), f32),
-        pltpu.VMEM((2, tokens, 128), f32),
         pltpu.VMEM((n, 8, 128), f32),
         pltpu.VMEM((n, 8, 128), f32),
         pltpu.VMEM((n, 8, 128), f32),
@@ -617,20 +627,19 @@
         pltpu.VMEM((n, 128, 128), bf16),
         pltpu.VMEM((n, 128, 128), bf16),
         pltpu.VMEM((n, 8, 128), f32),
-        pltpu.VMEM((rows * chips, 128), f32),
-        pltpu.VMEM((rows * chips, 128), bf16),
-        pltpu.VMEM((rows * chips, 128), bf16),
-        pltpu.VMEM((chips, rows, 128), bf16),
-        pltpu.VMEM((chips, rows, 128), bf16),
-        pltpu.VMEM((nz, rows, 128), bf16),
+        pltpu.VMEM((GS * FT, cols), bf16),
+        pltpu.VMEM((64, GS * FT), bf16),
+        pltpu.VMEM((64, cols), bf16),
+        pltpu.VMEM((gx, rows, cols), bf16),
+        pltpu.VMEM((nz, rows, cols), bf16),
         sems((16,)),
-        sems((26,)),
+        sems((28,)),
     ]
     dmd, wg = pl.pallas_call(
         functools.partial(kernel, n, nz, blk),
         out_shape=(
             jax.ShapeDtypeStruct((1, 64, FT), f32),
-            jax.ShapeDtypeStruct((2, chips, rows, 128), bf16),
+            jax.ShapeDtypeStruct((64, d), bf16),
         ),
         in_specs=[pl.BlockSpec(memory_space=pltpu.SMEM)] + [vm] * 4 + [hbm] * 16,
         out_specs=(vm, vm),
@@ -646,8 +655,7 @@
         out_real, out_fake,
         query_real, key_real, value_real, query_fake, key_fake, value_fake,
     )
-    wg = wg.reshape(d // 128, 64, 128).transpose(1, 0, 2).reshape(64, d).astype(f32)
-    return dmd, wg
+    return dmd, wg.astype(f32)
 
 
 def solution(mesh):

time: 108 us -> 98.4 us (0.911)
  Pallas kernels: 102 us -> 92.8 us
    pallas_call x1, Pallas kernels: 102 us -> 92.8 us  [per_device(): pl.pallas_call(functools.partial(kernel, n, nz, blk), out_shape=(jax.Shap...]
where the time goes in v3:
time: 98.4 us; the launch traced here: 98.2 us
  Pallas kernels  92.8 us (94%)
  other arithmetic  2.8 us (3%)
  between operations  1.35 us (1%)
  local copies, waits for them, and re-layouts  1.29 us (1%)
    pallas_call x1, Pallas kernels, per_device(): pl.pallas_call(functools.partial(kernel, n, nz, blk), out_shape=(jax.Shap...  92.8 us
    convert_element_type x1, other arithmetic, per_device(): return (dmd, wg.astype(f32))  2.23 us

profile of v3, /device:TPU:1, one launch (start us, length us, event | category | flops | bytes accessed | tf_op | source)
XLA Modules:
  0.0 98.2 jit_solution(640687419758257232)
XLA Ops:
  1.3 0.5 compare_select_fusion.4.sc
  1.8 0.1 fusion.1
  1.9 0.7 broadcast_in_dim.21.wave
  2.6 92.8 %dmd.1 = (f32[1,64,128]{2,1,0:T(8,128)}, bf16[64,5120]{1,0:T(8,128)(2,1)}) custom-call(f32[8]{0:T(128)} %compare_select_fusion.4.sc, f32[8,128]{1,0:T(8,128)} %broadcast_in_dim.21.wave, bf16[1,64,128]{2,1,0:T(8,128)(2,1)} %noise.1, f32[2,128]{1,0:T(2,128)} %gain_r.1, f32[2,128]{1,0:T(2,128)} %gain_f.1, bf16[3,8,5120]{2,1,0:T(8,128)(2,1)} %bitcast.3, ...), custom_call_target="tpu_custom_call" | custom-call | tf_op jit(solution)/shard_map/dmd/pallas_call | solution.py:638
  95.4 0.0 copy-start
  95.4 2.2 %convert_element_type.35 = f32[64,5120]{1,0:T(8,128)} convert(bf16[64,5120]{1,0:T(8,128)(2,1)} %get-tuple-element.5) | non-fusion elementwise | flops 327680 | bytes 1966080 | tf_op jit(solution)/shard_map/convert_element_type | solution.py:658
  97.6 0.0 copy-done
  97.6 0.6 copy.24
Async XLA Ops:
  95.4 2.2 %copy-start = (f32[1,64,128]{2,1,0:T(8,128)S(1)}, f32[1,64,128]{2,1,0:T(8,128)}, u32[]{:S(2)}) copy-start(f32[1,64,128]{2,1,0:T(8,128)} %get-tuple-element.8) | copy-start | bytes 98308

commit v4 on v3

--- a/solution.py
+++ b/solution.py
@@ -53,46 +53,60 @@
             self.now.__enter__()
 
 
-def attend_block(block, blk, tokens, qt_ref, k_ref, v_ref, m_ref, o_ref, s_ref):
-    q_at = pl.multiple_of(block * blk, blk)
+def attend_block(block, later, blk, qt_ref, k_ref, v_ref, m_ref, o_ref, s_ref):
     frames = blk // FT
 
-    def score(net, k_at):
+    def score(net, k_block, q_block):
+        k_at = pl.multiple_of(k_block * blk, blk)
+        q_at = pl.multiple_of(q_block * blk, blk)
         return mm(k_ref[net, pl.ds(k_at, blk), :], qt_ref[net, :, pl.ds(q_at, blk)])
 
-    for net in range(2):
-        s_ref[net] = score(net, 0)
-    for net in range(2):
-        s = score(net, q_at)
-        rows = []
-        for r in range(frames):
-            part = s[r * FT : (r + 1) * FT]
-            if r:
-                gone = jnp.full((FT, r * FT), -1e30, f32)
-                part = jnp.concatenate([gone, part[:, r * FT :]], axis=1)
-            rows.append(part)
-        s = jnp.concatenate(rows, axis=0)
-        top = jnp.max(s, axis=0, keepdims=True)
-        p = jnp.exp2(s - top).astype(bf16)
-        m_ref[net] = jnp.broadcast_to(top, (8, blk))
-        o_ref[net] = mm(v_ref[net, :, pl.ds(q_at, blk)], p)
-
-    def step(kb, _):
+    if later is None:
+        for net in range(2):
+            s_ref[net] = score(net, block, block)
+        return
+
+    def advance(kb, last, first):
+        next_k = jnp.where(last, later, 0 if first else kb + 1)
+        next_q = jnp.where(last, later, block)
         k_at = pl.multiple_of(kb * blk, blk)
-        next_at = pl.multiple_of(jnp.minimum(kb + 1, tokens // blk - 1) * blk, blk)
         for net in range(2):
             s = s_ref[net]
-            old = m_ref[net, 0:1, :]
-            top = jnp.maximum(old, jnp.max(s, axis=0, keepdims=True))
+            if first:
+                rows = []
+                for r in range(frames):
+                    part = s[r * FT : (r + 1) * FT]
+                    if r:
+                        gone = jnp.full((FT, r * FT), -1e30, f32)
+                        part = jnp.concatenate([gone, part[:, r * FT :]], axis=1)
+                    rows.append(part)
+                s = jnp.concatenate(rows, axis=0)
+            top = jnp.max(s, axis=0, keepdims=True)
+            if not first:
+                old = m_ref[net, 0:1, :]
+                top = jnp.maximum(old, top)
             p = jnp.exp2(s - top).astype(bf16)
-            ahead = score(net, next_at)
-            fade = jnp.exp2(old - top)
-            o_ref[net] = o_ref[net] * fade + mm(v_ref[net, :, pl.ds(k_at, blk)], p)
+            s_ref[net] = score(net, next_k, next_q)
+            o = mm(v_ref[net, :, pl.ds(k_at, blk)], p)
+            if not first:
+                o = o_ref[net] * jnp.exp2(old - top) + o
+            o_ref[net] = o
             m_ref[net] = jnp.broadcast_to(top, (8, blk))
-            s_ref[net] = ahead
-        return 0
-
-    lax.fori_loop(0, block, step, 0)
+
+    advance(block, block == 0, True)
+
+    def pair(i, _):
+        for u in range(2):
+            kb = i * 2 + u
+            advance(kb, kb == block - 1, False)
+        return 0
+
+    def single(kb, _):
+        advance(kb, kb == block - 1, False)
+        return 0
+
+    lax.fori_loop(0, block // 2, pair, 0)
+    lax.fori_loop(block // 2 * 2, block, single, 0)
 
 
 def block_at(s, me, per, blocks):
@@ -108,12 +122,12 @@
 
 def kernel(
     n, nz, blk,
-    sc, wave, noise, gain_r, gain_f,
-    time_rh, time_fh, hidden_h, genw_h, emb_rh, emb_fh, proj_rh, proj_fh, out_rh, out_fh,
+    step_ref,
+    noise_h, gain_rh, gain_fh, time_rh, time_fh, hidden_h, genw_h, emb_rh, emb_fh, proj_rh, proj_fh, out_rh, out_fh,
     wq_r, wk_r, wv_r, wq_f, wk_f, wv_f,
     dmd_ref, wg_ref,
-    times, hid, genw, emb, proj, outw, wqk, wv,
-    modbuf, modin, modfull, xg, xs, gen_s, mu_s, gmat, rmat,
+    noise, gain, times, hid, genw, emb, proj, outw, wqk, wv,
+    modbuf, modout, modin, modall, modfull, xg, xs, gen_s, mu_s, gmat, rmat,
     lhs, acc, lhs2, acc2, accv, rs_s, qraw, kraw, nbuf, nin, nfull,
     qt, kn, vt, m_s, o_s, s_s,
     tsend, trecv, gapbuf, hcol, dcat, wsend, wrecv, zbuf,
@@ -138,6 +152,7 @@
         return c
 
     ld_time = [load(time_rh, times.at[0]), load(time_fh, times.at[1])]
+    ld_noise = load(noise_h.at[0], noise)
     ld_hid = load(hidden_h.at[0], hid)
     ld_gen = load(genw_h, genw)
     ld_emb = [load(emb_rh, emb.at[0]), load(emb_fh, emb.at[1])]
@@ -149,6 +164,8 @@
     ld_v = [load(wv_r, wv.at[0]), load(wv_f, wv.at[1])]
     ld_out = [load(out_rh, outw.at[0]), load(out_fh, outw.at[1])]
 
+    ld_gain = [load(gain_rh, gain.at[0]), load(gain_fh, gain.at[1])]
+
     barrier = pltpu.get_barrier_semaphore()
 
     def greet(i, _):
@@ -198,42 +215,108 @@
             c.wait_recv()
             c.wait_send()
 
+        def owners(self, src_of, dst, count):
+            def body(i, _):
+                j = lax.rem(chip + i, chips)
+
+                @pl.when(jnp.logical_and(j < count, 2 * j + 1 != me))
+                def _():
+                    self.to(src_of(j), dst, 2 * j + 1).start()
+
+                return 0
+
+            lax.fori_loop(0, chips, body, 0)
+
+        def to_owner(self, whole, count, then):
+            owner = jnp.logical_and(core == 1, chip < count)
+
+            @pl.when(owner)
+            def _():
+                self.to(whole, whole, other).wait_recv()
+                then()
+
+                def body(i, _):
+                    j = lax.rem(me + i, n)
+                    self.back.to(self.result, self.result, j).start()
+                    return 0
+
+                lax.fori_loop(1, n, body, 0)
+
+            return owner
+
+        def settle(self, owner, sent, fewer):
+            @pl.when(owner)
+            def _():
+                self.to(fewer, fewer, other).wait_send()
+
+            @pl.when(jnp.logical_not(owner))
+            def _():
+                self.to(sent, sent, other).wait_send()
+
+        def gather(self, owner, whole, all_in, fewer):
+            @pl.when(owner)
+            def _():
+                self.to(whole, whole, other).wait_send()
+                self.to(fewer, fewer, other).wait_recv()
+
+            @pl.when(jnp.logical_not(owner))
+            def _():
+                self.to(all_in, all_in, other).wait_recv()
+
+    pieces = (6 * groups + 1) // 2
     mod_rs, mod_ag, xl, xf = Lane(), Lane(), Lane(), Lane()
     nrm_rs, nrm_ag, tl, gl = Lane(), Lane(), Lane(), Lane()
     hl, dl, w_rs, w_z, w_ag, w_fw = Lane(), Lane(), Lane(), Lane(), Lane(), Lane()
-    member = lax.rem(me, GS)
-    home = me - member
-    gx = n // GS
-    myx = me // GS
+    gy = GS // 2
+    half_d = d // 2
+    slot = pl.ds(pl.multiple_of(core * FT, FT), FT)
+
+    def half_of(c):
+        return pl.ds(pl.multiple_of(c * half_d, 128), half_d)
+
 
     ph("share")
-    for p in range(6 * groups, n):
+    step = jnp.full((1, 128), step_ref[0], jnp.int32).astype(f32)
+    raw = step / 1000.0
+    sigma = 5.0 * raw / (1.0 + 4.0 * raw)
+    freqs = times.shape[2]
+    first = me * freqs + lax.broadcasted_iota(jnp.int32, (freqs, 128), 0)
+    k = lax.rem(first, FREQ // 2).astype(f32)
+    angle = step * jnp.exp(k * (-math.log(10000.0) / (FREQ // 2)))
+    turns = jnp.floor(angle * (0.5 / math.pi) + 0.5)
+    angle = (angle - turns * 6.28125) - turns * (2.0 * math.pi - 6.28125)
+    wave = jnp.where(first < FREQ // 2, jnp.cos(angle), jnp.sin(angle)).astype(bf16).astype(f32)
+    for p in range(6 * groups, 2 * pieces):
         modbuf[p] = jnp.zeros((8, 128), f32)
     for net in range(2):
         ld_time[net].wait()
         for c in range(3):
             for b in range(8 * groups):
                 t = times[net, c, :, b * 128 : (b + 1) * 128].astype(f32)
-                part = jnp.sum(t * wave[...], axis=0, keepdims=True)
+                part = jnp.sum(t * wave, axis=0, keepdims=True)
                 modbuf[(net * 3 + c) * groups + b // 8, b % 8 : b % 8 + 1, :] = part
-    modin[me] = modbuf[me]
-
+    for j in range(pieces):
+        pair = jnp.concatenate([modbuf[2 * j], modbuf[2 * j + 1]], axis=0)
+        modout[j] = pair.astype(bf16)
     ph("barrier")
     pl.semaphore_wait(barrier, n - 1 + nz - 1)
-    mod_rs.all(lambda j: modbuf.at[j], modin.at[me])
+    mod_rs.owners(lambda j: modout.at[j], modin.at[me], pieces)
 
     ph("generate")
     ld_hid.wait()
     ld_gen.wait()
     generated = mm_t(genw[...], hid[...]).astype(bf16)
     gen_s[...] = generated
-    xg[chip, core] = (sc[1] * generated.astype(f32) + sc[0] * noise[0].astype(f32)).astype(bf16)
+    ld_noise.wait()
+    mixed = (1.0 - sigma) * generated.astype(f32) + sigma * noise[...].astype(f32)
+    xg[chip, core] = mixed.astype(bf16)
     mine = xg.at[chip, core]
     xl.mates(lambda j: mine, mine)
 
     ph("weights")
     ones_k = jnp.ones((1024, 128), bf16)
-    for net in range(2):
+
+    def weight_terms(net):
         ld_emb[net].wait()
         ld_proj[net].wait()
 
@@ -253,14 +336,28 @@
         gmat[net] = stack2(ee / d - mu * mu.T)
         rmat[net] = stack2(rr)
 
+    weight_terms(0)
     ph("mod_rs")
-    mod_rs.wait(modin.at[pl.ds(0, n - 1)])
-    modfull[me] = jnp.sum(modin[...], axis=0)
-    mod_ag.all(lambda j: modfull.at[me], modfull.at[me])
+
+    def add_mod():
+        modin[me] = modout[chip]
+        total = modin[0].astype(f32)
+        for j in range(1, n):
+            total = total + modin[j].astype(f32)
+        modall[chip] = total.astype(bf16)
+
+    mod_rs.back, mod_rs.result = mod_ag, modall.at[chip]
+    mod_owner = mod_rs.to_owner(modin.at[pl.ds(0, n - 1)], pieces, add_mod)
+    mod_rs.settle(mod_owner, modout.at[pl.ds(0, pieces)], modout.at[pl.ds(0, pieces - 1)])
+    hl.to(hid.at[:, half_of(1 - core)], hcol.at[slot, :], other).start()
 
     ph("x_wait")
     xl.wait(xg.at[pl.ds(0, chips - 1), core])
     xf.to(xg.at[:, core], xg.at[:, core], other).start()
+    ph("weights1")
+    weight_terms(1)
+    hcol[slot, :] = hid[:, half_of(core)]
+    ph("x_fwait")
     xf.wait(xg.at[:, core])
 
     ph("place_var")
@@ -295,7 +392,14 @@
     for c in ld_qk:
         c.wait()
     ph("mod_ag_wait")
-    mod_ag.wait(modfull.at[pl.ds(0, n - 1)])
+    mod_ag.gather(
+        mod_owner, modin.at[pl.ds(0, n - 1)], modall.at[pl.ds(0, pieces)],
+        modall.at[pl.ds(0, pieces - 1)],
+    )
+    for j in range(pieces):
+        both = modall[j].astype(f32)
+        modfull[2 * j] = both[0:8]
+        modfull[2 * j + 1] = both[8:16]
 
     ph("qk_fold")
     row = lax.broadcasted_iota(jnp.int32, (16, 128), 0)
@@ -339,7 +443,8 @@
                 dst[net, :, pl.ds(at, width)] = y
                 sq = jnp.sum(y * y, axis=0, keepdims=True)
                 for r in range(width // FT):
-                    nbuf[t * (width // FT) + r, net * 2 + which : net * 2 + which + 1, :] = sq[
+                    row = (r % 2) * 4 + net * 2 + which
+                    nbuf[t * (width // FT // 2) + r // 2, row : row + 1, :] = sq[
                         :, r * FT : (r + 1) * FT
                     ]
         return 0
@@ -347,8 +452,7 @@
     lax.fori_loop(0, tokens // width, project, 0, unroll=2)
 
     ph("norm_send")
-    nin[me] = nbuf[me]
-    nrm_rs.all(lambda j: nbuf.at[j], nin.at[me])
+    nrm_rs.owners(lambda j: nbuf.at[j], nin.at[me], chips)
 
     ph("v_fold")
     for c in ld_v + ld_out:
@@ -373,9 +477,14 @@
     lax.fori_loop(0, groups, fold_v, 0)
 
     ph("norm_rs_wait")
-    nrm_rs.wait(nin.at[pl.ds(0, n - 1)])
-    nfull[me] = lax.rsqrt(jnp.sum(nin[...], axis=0) / float(n * HD) + norm_floor)
-    nrm_ag.all(lambda j: nfull.at[me], nfull.at[me])
+
+    def add_norm():
+        nin[me] = nbuf[chip]
+        nfull[chip] = lax.rsqrt(jnp.sum(nin[...], axis=0) / float(n * HD) + norm_floor)
+
+    nrm_rs.back, nrm_rs.result = nrm_ag, nfull.at[chip]
+    nrm_owner = nrm_rs.to_owner(nin.at[pl.ds(0, n - 1)], chips, add_norm)
+    nrm_rs.settle(nrm_owner, nbuf.at[pl.ds(0, chips)], nbuf.at[pl.ds(0, chips - 1)])
 
     ph("values")
     vmats = []
@@ -403,15 +512,27 @@
 
     lax.fori_loop(0, tokens // width, values, 0, unroll=2)
     gains = []
-    for gain in (gain_r, gain_f):
-        both = gain[0:1, :] * gain[1:2, :] * (math.log2(math.e) / math.sqrt(HD))
+    for net in range(2):
+        ld_gain[net].wait()
+        both = gain[net, 0:1, :] * gain[net, 1:2, :] * (math.log2(math.e) / math.sqrt(HD))
         gains.append(jnp.broadcast_to(both, (128, 128)).T)
+
+    def gained(t, _):
+        at = pl.multiple_of(t * FT, FT)
+        for net in range(2):
+            qraw[net, :, pl.ds(at, FT)] = qraw[net, :, pl.ds(at, FT)] * gains[net]
+        return 0
+
+    lax.fori_loop(0, n, gained, 0, unroll=4)
     same = lax.broadcasted_iota(jnp.int32, (256, 256), 0) == lax.broadcasted_iota(
         jnp.int32, (256, 256), 1
     )
     eye = jnp.where(same, 1.0, 0.0).astype(bf16)
     ph("norm_ag_wait")
-    nrm_ag.wait(nfull.at[pl.ds(0, n - 1)])
+    nrm_ag.gather(
+        nrm_owner, nin.at[pl.ds(0, n - 1)], nfull.at[pl.ds(0, chips)],
+        nfull.at[pl.ds(0, chips - 1)],
+    )
 
     ph("normalise")
 
@@ -421,11 +542,12 @@
         for net in range(2):
             k_cols = []
             for half in range(2):
-                scales = nfull[t * 2 + half]
+                scales = nfull[t]
                 to = pl.ds(pl.multiple_of(at + half * FT, FT), FT)
-                sq = scales[net * 2 : net * 2 + 1, :]
-                sk = scales[net * 2 + 1 : net * 2 + 2, :]
-                qt[net, :, to] = (qraw[net, :, to] * sq * gains[net]).astype(bf16)
+                at_row = half * 4 + net * 2
+                sq = scales[at_row : at_row + 1, :]
+                sk = scales[at_row + 1 : at_row + 2, :]
+                qt[net, :, to] = (qraw[net, :, to] * sq).astype(bf16)
                 k_cols.append((kraw[net, :, to] * sk).astype(bf16))
             k_rows.append(jnp.concatenate(k_cols, axis=1))
         turned = mm_t(eye, jnp.concatenate(k_rows, axis=0)).astype(bf16)
@@ -433,18 +555,7 @@
             kn[net, pl.ds(at, 256), :] = turned[:, net * HD : (net + 1) * HD]
         return 0
 
-    lax.fori_loop(0, tokens // 256, normalise, 0, unroll=2)
-
-    def share_cols(i, _):
-        j = lax.rem(member + i, GS)
-        src = hid.at[:, pl.ds(pl.multiple_of(j * hcol.shape[1], 128), hcol.shape[1])]
-        hl.to(src, hcol.at[pl.ds(pl.multiple_of(member * FT, FT), FT), :], home + j).start()
-        return 0
-
-    lax.fori_loop(1, GS, share_cols, 0)
-    hcol[pl.ds(pl.multiple_of(member * FT, FT), FT), :] = hid[
-        :, pl.ds(pl.multiple_of(member * hcol.shape[1], 128), hcol.shape[1])
-    ]
+    lax.fori_loop(0, tokens // 256, normalise, 0, unroll=4)
 
     ph("attend")
     blocks = tokens // blk
@@ -452,7 +563,8 @@
 
     def one_block(s, _):
         block = block_at(s, me, per, blocks)
-        attend_block(block, blk, tokens, qt, kn, vt, m_s, o_s, s_s)
+        later = block_at(lax.rem(s + 1, blocks), me, per, blocks)
+        attend_block(block, later, blk, qt, kn, vt, m_s, o_s, s_s)
         for net in range(2):
             o = o_s[net]
             y = (o[0:64] / o[64:65]).astype(bf16)
@@ -467,6 +579,7 @@
 
         return 0
 
+    attend_block(block_at(0, me, per, blocks), None, blk, qt, kn, vt, m_s, o_s, s_s)
     lax.fori_loop(0, blocks, one_block, 0)
     ph("t_wait")
     x_own = xs[:, pl.ds(pl.multiple_of(me * FT, FT), FT)]
@@ -484,50 +597,46 @@
     vel = lax.fori_loop(0, n, add_up, jnp.zeros((128, FT), f32), unroll=8)
     vel_r = vel[0:64] + base_r[0:64] + base_r[64:128]
     vel_f = vel[64:128] + base_f[0:64] + base_f[64:128]
-    pred_r = noisy - sc[0] * vel_r
-    pred_f = noisy - sc[0] * vel_f
+    pred_r = noisy - sigma * vel_r
+    pred_f = noisy - sigma * vel_f
     gap = jnp.abs(gen_s[...].astype(f32) - pred_r)
     gsum = gap[0:8]
     for r in range(1, 8):
         gsum = gsum + gap[r * 8 : (r + 1) * 8]
     gapbuf[me] = gsum
     diff = pred_f - pred_r
-    own = dcat.at[:, pl.ds(pl.multiple_of(member * FT, FT), FT)]
+    own = dcat.at[:, slot]
     own[...] = diff.astype(bf16)
-
-    def share_diff(i, _):
-        dl.to(own, own, home + lax.rem(member + i, GS)).start()
-        return 0
-
-    lax.fori_loop(1, GS, share_diff, 0)
+    dl.to(own, own, other).start()
     gl.all(lambda j: gapbuf.at[me], gapbuf.at[me])
     dmd_ref[0] = diff
     ph("h_wait")
-    hl.wait(hcol.at[pl.ds(0, (GS - 1) * FT), :])
+    hl.wait(hcol.at[pl.ds(0, FT), :])
     ph("d_wait")
-    dl.wait(dcat.at[:, pl.ds(0, (GS - 1) * FT)])
+    dl.wait(dcat.at[:, pl.ds(0, FT)])
     ph("wg_mm")
     wsend[...] = mm(dcat[...], hcol[...]).astype(bf16)
     rows = wrecv.shape[1]
-
-    def x_rows(x):
-        return pl.ds(pl.multiple_of(x * rows, 16), rows)
-
-    for i in range(1, gx):
-        x = lax.rem(myx + i, gx)
-        w_rs.to(wsend.at[x_rows(x), :], wrecv.at[myx], x * GS + member).start()
-    wrecv[myx] = wsend[x_rows(myx), :]
+    cols = wrecv.shape[2]
+
+    def piece(j, c):
+        return (
+            pl.ds(pl.multiple_of(j // gy * rows, 16), rows),
+            pl.ds(pl.multiple_of(c * half_d + lax.rem(j, gy) * cols, 128), cols),
+        )
+
+    w_rs.mates(lambda j: wsend.at[piece(j, 0)], wrecv.at[chip])
+    wrecv[chip] = wsend[piece(chip, 0)]
     ph("gap_wait")
     gl.wait(gapbuf.at[pl.ds(0, n - 1)])
     gap_all = jnp.sum(jnp.sum(gapbuf[...], axis=0), keepdims=True)
     inv = 1.0 / jnp.maximum(gap_all / (64.0 * tokens), gap_floor)
     dmd_ref[0] = dmd_ref[0] * inv
     ph("w_wait")
-    if gx > 1:
-        w_rs.wait(wrecv.at[pl.ds(0, gx - 1)])
+    w_rs.wait(wrecv.at[pl.ds(0, chips - 1)])
     wsum = wrecv[0].astype(f32)
-    for x in range(1, gx):
-        wsum = wsum + wrecv[x].astype(f32)
+    for j in range(1, chips):
+        wsum = wsum + wrecv[j].astype(f32)
     zbuf[mz] = (wsum * (inv / math.sqrt(nz * tokens))).astype(bf16)
     ph("w_z")
     for i in range(1, nz):
@@ -541,21 +650,14 @@
     for z in range(1, nz):
         whole = whole + zbuf[z].astype(f32)
     ph("w_ag")
-    cols = wrecv.shape[2]
-
-    def col(g):
-        return pl.ds(pl.multiple_of(g * cols, 128), cols)
-
-    part = wg_ref.at[x_rows(myx), col(member)]
+    part = wg_ref.at[piece(chip, core)]
     part[...] = whole.astype(bf16)
     w_ag.mates(lambda j: part, part)
-    fold_by = next(k for k in range(1, chips) if (chips - 1) % k == 0 and (chips - 1) // k <= GS)
-    w_ag.wait(wg_ref.at[pl.ds(0, fold_by * rows), pl.ds(0, (chips - 1) // fold_by * cols)])
+    w_ag.wait(wrecv.at[pl.ds(0, chips - 1)])
     ph("w_forward")
-    for y in range(GS // 2):
-        view = wg_ref.at[:, col(2 * y + core)]
-        w_fw.to(view, view, other).start()
-    w_fw.wait(wg_ref.at[:, pl.ds(0, d // 2)])
+    mine_half = wg_ref.at[:, half_of(core)]
+    w_fw.to(mine_half, mine_half, other).start()
+    w_fw.wait(mine_half)
     ph(None)
 
 
@@ -570,26 +672,15 @@
     tokens = n * FT
     blk = 512
     chips = n // 2
-    gx = n // GS
-    rows = 64 // gx
+    rows = 64 // (n // GS)
     cols = d // GS
     fr = time_real.shape[0]
-    step = timesteps[0].astype(f32)
-    raw = step / 1000.0
-    sigma = 5.0 * raw / (1.0 + 4.0 * raw)
-    half = FREQ // 2
-    at = lax.axis_index("tm") * fr + jnp.arange(fr, dtype=jnp.int32)
-    freq = jnp.exp(-math.log(10000.0) * (at % half).astype(f32) / half)
-    wave = jnp.where(at < half, jnp.cos(step * freq), jnp.sin(step * freq))
-    wave = wave.astype(bf16).astype(f32)
-    wave = jnp.broadcast_to(wave[:, None], (fr, 128))
-    slot = jnp.arange(8)
-    sc = jnp.where(slot == 0, sigma, jnp.where(slot == 1, 1.0 - sigma, 0.0))
-
     vm = pl.BlockSpec(memory_space=pltpu.VMEM)
     hbm = pl.BlockSpec(memory_space=pl.ANY)
     sems = pltpu.SemaphoreType.DMA
     scratch = [
+        pltpu.VMEM((64, FT), bf16),
+        pltpu.VMEM((2, 2, HD), f32),
         pltpu.VMEM((2, 3, fr, d), bf16),
         pltpu.VMEM((FT, d), bf16),
         pltpu.VMEM((64, d), bf16),
@@ -599,7 +690,9 @@
         pltpu.VMEM((2, d, 256), bf16),
         pltpu.VMEM((2, d, 128), bf16),
         pltpu.VMEM((n, 8, 128), f32),
-        pltpu.VMEM((n, 8, 128), f32),
+        pltpu.VMEM((chips, 16, 128), bf16),
+        pltpu.VMEM((n, 16, 128), bf16),
+        pltpu.VMEM((chips, 16, 128), bf16),
         pltpu.VMEM((n, 8, 128), f32),
         pltpu.VMEM((chips, 2, 64, 128), bf16),
         pltpu.VMEM((128, tokens), bf16),
@@ -615,9 +708,9 @@
         pltpu.VMEM((2, 8, tokens), f32),
         pltpu.VMEM((2, 128, tokens), f32),
         pltpu.VMEM((2, 128, tokens), f32),
+        pltpu.VMEM((chips, 8, 128), f32),
         pltpu.VMEM((n, 8, 128), f32),
-        pltpu.VMEM((n, 8, 128), f32),
-        pltpu.VMEM((n, 8, 128), f32),
+        pltpu.VMEM((chips, 8, 128), f32),
         pltpu.VMEM((2, 128, tokens), bf16),
         pltpu.VMEM((2, tokens, 128), bf16),
         pltpu.VMEM((2, 80, tokens), bf16),
@@ -627,12 +720,12 @@
         pltpu.VMEM((n, 128, 128), bf16),
         pltpu.VMEM((n, 128, 128), bf16),
         pltpu.VMEM((n, 8, 128), f32),
-        pltpu.VMEM((GS * FT, cols), bf16),
-        pltpu.VMEM((64, GS * FT), bf16),
-        pltpu.VMEM((64, cols), bf16),
-        pltpu.VMEM((gx, rows, cols), bf16),
+        pltpu.VMEM((2 * FT, d // 2), bf16),
+        pltpu.VMEM((64, 2 * FT), bf16),
+        pltpu.VMEM((64, d // 2), bf16),
+        pltpu.VMEM((chips, rows, cols), bf16),
         pltpu.VMEM((nz, rows, cols), bf16),
-        sems((16,)),
+        sems((20,)),
         sems((28,)),
     ]
     dmd, wg = pl.pallas_call(
@@ -641,7 +734,7 @@
             jax.ShapeDtypeStruct((1, 64, FT), f32),
             jax.ShapeDtypeStruct((64, d), bf16),
         ),
-        in_specs=[pl.BlockSpec(memory_space=pltpu.SMEM)] + [vm] * 4 + [hbm] * 16,
+        in_specs=[pl.BlockSpec(memory_space=pltpu.SMEM)] + [hbm] * 19,
         out_specs=(vm, vm),
         scratch_shapes=scratch,
         compiler_params=pltpu.CompilerParams(
@@ -649,7 +742,7 @@
         ),
         name="dmd",
     )(
-        sc, wave, noise_field, gain_real, gain_fake,
+        timesteps, noise_field, gain_real, gain_fake,
         time_real.transpose(1, 0, 2), time_fake.transpose(1, 0, 2),
         hidden_states, gen_weight, embed_real, embed_fake, proj_real, proj_fake,
         out_real, out_fake,

time: 98.4 us -> 88.2 us (0.90)
  Pallas kernels: 92.8 us -> 83.9 us
    pallas_call x1, Pallas kernels: 92.8 us -> 83.9 us  [per_device(): pl.pallas_call(functools.partial(kernel, n, nz, blk), out_shape=(jax.Shap...]
where the time goes in v4:
time: 88.2 us; the launch traced here: 88 us
  Pallas kernels  83.9 us (95%)
  other arithmetic  2.23 us (3%)
  between operations  1.3 us (1%)
    pallas_call x1, Pallas kernels, per_device(): pl.pallas_call(functools.partial(kernel, n, nz, blk), out_shape=(jax.Shap...  83.9 us
    convert_element_type x1, other arithmetic, per_device(): return (dmd, wg.astype(f32))  2.23 us

profile of v4, /device:TPU:1, one launch (start us, length us, event | category | flops | bytes accessed | tf_op | source)
XLA Modules:
  0.0 88.0 jit_solution(9990908970624957871)
XLA Ops:
  1.3 83.9 %dmd.1 = (f32[1,64,128]{2,1,0:T(8,128)}, bf16[64,5120]{1,0:T(8,128)(2,1)}) custom-call(s32[1]{0:T(128)S(6)} %copy.23.step_ref, bf16[1,64,128]{2,1,0:T(8,128)(2,1)} %noise_h.1, f32[2,128]{1,0:T(2,128)} %gain_rh.1, f32[2,128]{1,0:T(2,128)} %gain_fh.1, bf16[3,8,5120]{2,1,0:T(8,128)(2,1)} %bitcast.2, bf16[3,8,5120]{2,1,0:T(8,128)(2,1)} %bitcast.3, ...), custom_call_target="tpu_custom_call" | custom-call | tf_op jit(solution)/shard_map/dmd/pallas_call | solution.py:731
  85.2 0.0 copy-start
  85.2 2.2 %convert_element_type.3 = f32[64,5120]{1,0:T(8,128)} convert(bf16[64,5120]{1,0:T(8,128)(2,1)} %get-tuple-element.5) | non-fusion elementwise | flops 327680 | bytes 1966080 | tf_op jit(solution)/shard_map/convert_element_type | solution.py:751
  87.4 0.0 copy-done
  87.4 0.6 copy.24
Async XLA Ops:
  85.2 2.2 %copy-start = (f32[1,64,128]{2,1,0:T(8,128)S(1)}, f32[1,64,128]{2,1,0:T(8,128)}, u32[]{:S(2)}) copy-start(f32[1,64,128]{2,1,0:T(8,128)} %get-tuple-element.8) | copy-start | bytes 98308

commit v5 on v4

--- a/solution.py
+++ b/solution.py
@@ -93,20 +93,24 @@
             o_ref[net] = o
             m_ref[net] = jnp.broadcast_to(top, (8, blk))
 
-    advance(block, block == 0, True)
+    odd = lax.rem(block, 2)
+
+    @pl.when(odd == 0)
+    def _():
+        advance(block, block == 0, True)
+
+    @pl.when(odd == 1)
+    def _():
+        advance(block, False, True)
+        advance(0, block == 1, False)
 
     def pair(i, _):
         for u in range(2):
-            kb = i * 2 + u
+            kb = odd + i * 2 + u
             advance(kb, kb == block - 1, False)
         return 0
 
-    def single(kb, _):
-        advance(kb, kb == block - 1, False)
-        return 0
-
     lax.fori_loop(0, block // 2, pair, 0)
-    lax.fori_loop(block // 2 * 2, block, single, 0)
 
 
 def block_at(s, me, per, blocks):
@@ -181,6 +185,12 @@
         )
 
     used = [0]
+    wide = chips // 4
+    shifts = [(dx, dy) for dx in range(wide) for dy in range(4) if dx or dy]
+    shifts.sort(key=lambda t: -min(t[0], wide - t[0]) - min(t[1], 4 - t[1]))
+    far_first = [
+        lax.rem(chip // 4 + dx, wide) * 4 + lax.rem(lax.rem(chip, 4) + dy, 4) for dx, dy in shifts
+    ]
 
     class Lane:
         def __init__(self):
@@ -203,12 +213,8 @@
             lax.fori_loop(1, n, body, 0)
 
         def mates(self, src_of, dst):
-            def body(i, _):
-                j = lax.rem(chip + i, chips)
+            for j in far_first:
                 self.to(src_of(j), dst, 2 * j + core).start()
-                return 0
-
-            lax.fori_loop(1, chips, body, 0)
 
         def wait(self, view):
             c = self.to(view, view, other)
@@ -216,16 +222,11 @@
             c.wait_send()
 
         def owners(self, src_of, dst, count):
-            def body(i, _):
-                j = lax.rem(chip + i, chips)
+            for j in far_first + [chip]:
 
                 @pl.when(jnp.logical_and(j < count, 2 * j + 1 != me))
                 def _():
                     self.to(src_of(j), dst, 2 * j + 1).start()
-
-                return 0
-
-            lax.fori_loop(0, chips, body, 0)
 
         def to_owner(self, whole, count, then):
             owner = jnp.logical_and(core == 1, chip < count)
@@ -235,12 +236,10 @@
                 self.to(whole, whole, other).wait_recv()
                 then()
 
-                def body(i, _):
-                    j = lax.rem(me + i, n)
-                    self.back.to(self.result, self.result, j).start()
-                    return 0
-
-                lax.fori_loop(1, n, body, 0)
+                for j in far_first:
+                    for c in range(2):
+                        self.back.to(self.result, self.result, 2 * j + c).start()
+                self.back.to(self.result, self.result, other).start()
 
             return owner
 
@@ -330,7 +329,9 @@
             )
 
         zero = jnp.zeros((128, 128), f32)
-        ee, mu, rr = lax.fori_loop(0, groups, gram, (zero, zero, jnp.zeros((64, 128), f32)))
+        ee, mu, rr = lax.fori_loop(
+            0, groups, gram, (zero, zero, jnp.zeros((64, 128), f32)), unroll=True
+        )
         mu = mu / d
         mu_s[net] = mu
         gmat[net] = stack2(ee / d - mu * mu.T)
@@ -351,30 +352,39 @@
     mod_rs.settle(mod_owner, modout.at[pl.ds(0, pieces)], modout.at[pl.ds(0, pieces - 1)])
     hl.to(hid.at[:, half_of(1 - core)], hcol.at[slot, :], other).start()
 
+    ph("weights1")
+    weight_terms(1)
+    hcol[slot, :] = hid[:, half_of(core)]
+
     ph("x_wait")
     xl.wait(xg.at[pl.ds(0, chips - 1), core])
     xf.to(xg.at[:, core], xg.at[:, core], other).start()
-    ph("weights1")
-    weight_terms(1)
-    hcol[slot, :] = hid[:, half_of(core)]
+    xs[64:128, 0:FT] = jnp.zeros((64, FT), bf16)
+
+    def place(parity, i):
+        at = pl.multiple_of(i * (2 * FT) + parity * FT, FT)
+        x = xg[i, parity]
+        xs[0:64, pl.ds(at, FT)] = x
+        return at, x
+
+    def place_both(parity):
+        def body(i, _):
+            at, x = place(parity, i)
+            xs[64:128, pl.ds(pl.multiple_of(at + FT, FT), FT)] = x
+            return 0
+
+        return body
+
+    lax.fori_loop(0, chips - 1, place_both(core), 0, unroll=5)
     ph("x_fwait")
     xf.wait(xg.at[:, core])
 
     ph("place_var")
 
-    def place(j, _):
-        at = pl.multiple_of(j * FT, FT)
-        xs[0:64, pl.ds(at, FT)] = xg[j // 2, lax.rem(j, 2)]
-        return 0
-
-    def place_late(j, _):
-        at = pl.multiple_of(j * FT + FT, FT)
-        xs[64:128, pl.ds(at, FT)] = xg[j // 2, lax.rem(j, 2)]
-        return 0
-
-    xs[64:128, 0:FT] = jnp.zeros((64, FT), bf16)
-    lax.fori_loop(0, n, place, 0, unroll=8)
-    lax.fori_loop(0, n - 1, place_late, 0, unroll=8)
+    lax.fori_loop(0, chips - 1, place_both(1 - core), 0, unroll=5)
+    at, x = place(0, chips - 1)
+    xs[64:128, pl.ds(pl.multiple_of(at + FT, FT), FT)] = x
+    place(1, chips - 1)
 
     width = blk
 
@@ -388,7 +398,7 @@
             rs_s[net, :, pl.ds(at, width)] = jnp.broadcast_to(rs, (8, width))
         return 0
 
-    lax.fori_loop(0, tokens // width, variances, 0, unroll=2)
+    lax.fori_loop(0, tokens // width, variances, 0, unroll=4)
     for c in ld_qk:
         c.wait()
     ph("mod_ag_wait")
@@ -422,7 +432,7 @@
             acc[net] += mm(lhs[net, :, pl.ds(at, 1024)], wqk[net, pl.ds(at, 1024), :])
         return 0
 
-    lax.fori_loop(0, groups, fold, 0)
+    lax.fori_loop(0, groups, fold, 0, unroll=True)
     ph("qk_project")
     mats = []
     for net in range(2):
@@ -449,7 +459,7 @@
                     ]
         return 0
 
-    lax.fori_loop(0, tokens // width, project, 0, unroll=2)
+    lax.fori_loop(0, tokens // width, project, 0, unroll=True)
 
     ph("norm_send")
     nrm_rs.owners(lambda j: nbuf.at[j], nin.at[me], chips)
@@ -474,7 +484,7 @@
             acc2[net] += mm_t(lhs2[net], outw[net, :, pl.ds(at, 1024)])
         return 0
 
-    lax.fori_loop(0, groups, fold_v, 0)
+    lax.fori_loop(0, groups, fold_v, 0, unroll=True)
 
     ph("norm_rs_wait")
 
@@ -510,7 +520,7 @@
             vt[net, 64:80, pl.ds(at, width)] = ones.astype(bf16)
         return 0
 
-    lax.fori_loop(0, tokens // width, values, 0, unroll=2)
+    lax.fori_loop(0, tokens // width, values, 0, unroll=4)
     gains = []
     for net in range(2):
         ld_gain[net].wait()
@@ -555,7 +565,7 @@
             kn[net, pl.ds(at, 256), :] = turned[:, net * HD : (net + 1) * HD]
         return 0
 
-    lax.fori_loop(0, tokens // 256, normalise, 0, unroll=4)
+    lax.fori_loop(0, tokens // 256, normalise, 0, unroll=True)
 
     ph("attend")
     blocks = tokens // blk
@@ -594,7 +604,7 @@
     def add_up(s, t):
         return t + trecv[s].astype(f32)
 
-    vel = lax.fori_loop(0, n, add_up, jnp.zeros((128, FT), f32), unroll=8)
+    vel = lax.fori_loop(0, n, add_up, jnp.zeros((128, FT), f32), unroll=True)
     vel_r = vel[0:64] + base_r[0:64] + base_r[64:128]
     vel_f = vel[64:128] + base_f[0:64] + base_f[64:128]
     pred_r = noisy - sigma * vel_r

time: 88.2 us -> 81.1 us (0.920)
  Pallas kernels: 83.9 us -> 76.8 us
    pallas_call x1, Pallas kernels: 83.9 us -> 76.8 us  [per_device(): pl.pallas_call(functools.partial(kernel, n, nz, blk), out_shape=(jax.Shap...]
where the time goes in v5:
time: 81.1 us; the launch traced here: 81 us
  Pallas kernels  76.8 us (95%)
  other arithmetic  2.23 us (3%)
  between operations  1.3 us (2%)
    pallas_call x1, Pallas kernels, per_device(): pl.pallas_call(functools.partial(kernel, n, nz, blk), out_shape=(jax.Shap...  76.8 us
    convert_element_type x1, other arithmetic, per_device(): return (dmd, wg.astype(f32))  2.23 us

profile of v5, /device:TPU:1, one launch (start us, length us, event | category | flops | bytes accessed | tf_op | source)
XLA Modules:
  0.0 81.0 jit_solution(12101828872218950563)
XLA Ops:
  1.3 76.8 %dmd.1 = (f32[1,64,128]{2,1,0:T(8,128)}, bf16[64,5120]{1,0:T(8,128)(2,1)}) custom-call(s32[1]{0:T(128)S(6)} %copy.23.step_ref, bf16[1,64,128]{2,1,0:T(8,128)(2,1)} %noise_h.1, f32[2,128]{1,0:T(2,128)} %gain_rh.1, f32[2,128]{1,0:T(2,128)} %gain_fh.1, bf16[3,8,5120]{2,1,0:T(8,128)(2,1)} %bitcast.2, bf16[3,8,5120]{2,1,0:T(8,128)(2,1)} %bitcast.3, ...), custom_call_target="tpu_custom_call" | custom-call | tf_op jit(solution)/shard_map/dmd/pallas_call | solution.py:741
  78.1 0.0 copy-start
  78.1 2.2 %convert_element_type.3 = f32[64,5120]{1,0:T(8,128)} convert(bf16[64,5120]{1,0:T(8,128)(2,1)} %get-tuple-element.5) | non-fusion elementwise | flops 327680 | bytes 1966080 | tf_op jit(solution)/shard_map/convert_element_type | solution.py:761
  80.4 0.0 copy-done
  80.4 0.6 copy.24
Async XLA Ops:
  78.1 2.2 %copy-start = (f32[1,64,128]{2,1,0:T(8,128)S(1)}, f32[1,64,128]{2,1,0:T(8,128)}, u32[]{:S(2)}) copy-start(f32[1,64,128]{2,1,0:T(8,128)} %get-tuple-element.8) | copy-start | bytes 98308

commit v6 on v5

--- a/solution.py
+++ b/solution.py
@@ -63,15 +63,15 @@
 
     if later is None:
         for net in range(2):
-            s_ref[net] = score(net, block, block)
+            s_ref[0, net] = score(net, block, block)
         return
 
-    def advance(kb, last, first):
+    def advance(kb, last, first, src, dst):
         next_k = jnp.where(last, later, 0 if first else kb + 1)
         next_q = jnp.where(last, later, block)
         k_at = pl.multiple_of(kb * blk, blk)
         for net in range(2):
-            s = s_ref[net]
+            s = s_ref[src, net]
             if first:
                 rows = []
                 for r in range(frames):
@@ -86,7 +86,7 @@
                 old = m_ref[net, 0:1, :]
                 top = jnp.maximum(old, top)
             p = jnp.exp2(s - top).astype(bf16)
-            s_ref[net] = score(net, next_k, next_q)
+            s_ref[dst, net] = score(net, next_k, next_q)
             o = mm(v_ref[net, :, pl.ds(k_at, blk)], p)
             if not first:
                 o = o_ref[net] * jnp.exp2(old - top) + o
@@ -97,17 +97,17 @@
 
     @pl.when(odd == 0)
     def _():
-        advance(block, block == 0, True)
+        advance(block, block == 0, True, 0, 0)
 
     @pl.when(odd == 1)
     def _():
-        advance(block, False, True)
-        advance(0, block == 1, False)
+        advance(block, False, True, 0, 1)
+        advance(0, block == 1, False, 1, 0)
 
     def pair(i, _):
         for u in range(2):
             kb = odd + i * 2 + u
-            advance(kb, kb == block - 1, False)
+            advance(kb, kb == block - 1, False, u, 1 - u)
         return 0
 
     lax.fori_loop(0, block // 2, pair, 0)
@@ -117,8 +117,8 @@
     home = me // per
     if blocks != 8:
         return lax.rem(home + 1 + s, blocks)
-    dx = jnp.where(s < 2, 2, jnp.where(s < 6, 1 + 2 * lax.rem(s - 2, 2), 0))
-    dy = jnp.where(s < 2, 1 - s, jnp.where(s < 4, 1, jnp.where(s < 6, 0, 7 - s)))
+    dx = jnp.where(s < 2, 2, jnp.where((s == 2) | (s == 7), 0, 1 + 2 * lax.rem(s - 1, 2)))
+    dy = jnp.where((s == 0) | ((s > 1) & (s < 5)), 1, 0)
     x = lax.rem(home // 2 + dx, 4)
     y = lax.rem(home + dy, 2)
     return x * 2 + y
@@ -129,12 +129,12 @@
     step_ref,
     noise_h, gain_rh, gain_fh, time_rh, time_fh, hidden_h, genw_h, emb_rh, emb_fh, proj_rh, proj_fh, out_rh, out_fh,
     wq_r, wk_r, wv_r, wq_f, wk_f, wv_f,
-    dmd_ref, wg_ref,
+    dmd_h, wg_h,
     noise, gain, times, hid, genw, emb, proj, outw, wqk, wv,
     modbuf, modout, modin, modall, modfull, xg, xs, gen_s, mu_s, gmat, rmat,
     lhs, acc, lhs2, acc2, accv, rs_s, qraw, kraw, nbuf, nin, nfull,
     qt, kn, vt, m_s, o_s, s_s,
-    tsend, trecv, gapbuf, hcol, dcat, wsend, wrecv, zbuf,
+    dmd_ref, wg_ref, tsend, trecv, gapbuf, hcol, dcat, wsend, wrecv, zbuf,
     lsem, sem,
 ):
     me = lax.axis_index("tm")
@@ -297,10 +297,6 @@
     for j in range(pieces):
         pair = jnp.concatenate([modbuf[2 * j], modbuf[2 * j + 1]], axis=0)
         modout[j] = pair.astype(bf16)
-    ph("barrier")
-    pl.semaphore_wait(barrier, n - 1 + nz - 1)
-    mod_rs.owners(lambda j: modout.at[j], modin.at[me], pieces)
-
     ph("generate")
     ld_hid.wait()
     ld_gen.wait()
@@ -309,6 +305,10 @@
     ld_noise.wait()
     mixed = (1.0 - sigma) * generated.astype(f32) + sigma * noise[...].astype(f32)
     xg[chip, core] = mixed.astype(bf16)
+    ph("barrier")
+    pl.semaphore_wait(barrier, n - 1 + nz - 1)
+    mod_rs.owners(lambda j: modout.at[j], modin.at[me], pieces)
+
     mine = xg.at[chip, core]
     xl.mates(lambda j: mine, mine)
 
@@ -350,7 +350,6 @@
     mod_rs.back, mod_rs.result = mod_ag, modall.at[chip]
     mod_owner = mod_rs.to_owner(modin.at[pl.ds(0, n - 1)], pieces, add_mod)
     mod_rs.settle(mod_owner, modout.at[pl.ds(0, pieces)], modout.at[pl.ds(0, pieces - 1)])
-    hl.to(hid.at[:, half_of(1 - core)], hcol.at[slot, :], other).start()
 
     ph("weights1")
     weight_terms(1)
@@ -378,6 +377,7 @@
     lax.fori_loop(0, chips - 1, place_both(core), 0, unroll=5)
     ph("x_fwait")
     xf.wait(xg.at[:, core])
+    hl.to(hid.at[:, half_of(1 - core)], hcol.at[slot, :], other).start()
 
     ph("place_var")
 
@@ -398,7 +398,7 @@
             rs_s[net, :, pl.ds(at, width)] = jnp.broadcast_to(rs, (8, width))
         return 0
 
-    lax.fori_loop(0, tokens // width, variances, 0, unroll=4)
+    lax.fori_loop(0, tokens // width, variances, 0, unroll=True)
     for c in ld_qk:
         c.wait()
     ph("mod_ag_wait")
@@ -613,13 +613,13 @@
     gsum = gap[0:8]
     for r in range(1, 8):
         gsum = gsum + gap[r * 8 : (r + 1) * 8]
-    gapbuf[me] = gsum
+    gapbuf[me] = jnp.sum(gsum, axis=0, keepdims=True)
     diff = pred_f - pred_r
     own = dcat.at[:, slot]
     own[...] = diff.astype(bf16)
     dl.to(own, own, other).start()
     gl.all(lambda j: gapbuf.at[me], gapbuf.at[me])
-    dmd_ref[0] = diff
+    dmd_ref[...] = diff
     ph("h_wait")
     hl.wait(hcol.at[pl.ds(0, FT), :])
     ph("d_wait")
@@ -641,7 +641,8 @@
     gl.wait(gapbuf.at[pl.ds(0, n - 1)])
     gap_all = jnp.sum(jnp.sum(gapbuf[...], axis=0), keepdims=True)
     inv = 1.0 / jnp.maximum(gap_all / (64.0 * tokens), gap_floor)
-    dmd_ref[0] = dmd_ref[0] * inv
+    dmd_ref[...] = dmd_ref[...] * inv
+    put_dmd = load(dmd_ref, dmd_h.at[0])
     ph("w_wait")
     w_rs.wait(wrecv.at[pl.ds(0, chips - 1)])
     wsum = wrecv[0].astype(f32)
@@ -665,9 +666,12 @@
     w_ag.mates(lambda j: part, part)
     w_ag.wait(wrecv.at[pl.ds(0, chips - 1)])
     ph("w_forward")
-    mine_half = wg_ref.at[:, half_of(core)]
-    w_fw.to(mine_half, mine_half, other).start()
-    w_fw.wait(mine_half)
+    w_fw.to(wg_ref.at[:, half_of(core)], wg_h.at[:, half_of(core)], other).start()
+    put_wg = load(wg_ref.at[:, half_of(core)], wg_h.at[:, half_of(core)])
+    put_dmd.wait()
+    put_wg.wait()
+    w_fw.to(wg_ref.at[:, half_of(core)], wg_h.at[:, half_of(1 - core)], other).wait_recv()
+    w_fw.to(wg_ref.at[:, half_of(core)], wg_h.at[:, half_of(core)], other).wait_send()
     ph(None)
 
 
@@ -685,7 +689,6 @@
     rows = 64 // (n // GS)
     cols = d // GS
     fr = time_real.shape[0]
-    vm = pl.BlockSpec(memory_space=pltpu.VMEM)
     hbm = pl.BlockSpec(memory_space=pl.ANY)
     sems = pltpu.SemaphoreType.DMA
     scratch = [
@@ -726,16 +729,18 @@
         pltpu.VMEM((2, 80, tokens), bf16),
         pltpu.VMEM((2, 8, blk), f32),
         pltpu.VMEM((2, 80, blk), f32),
-        pltpu.VMEM((2, blk, blk), f32),
+        pltpu.VMEM((2, 2, blk, blk), f32),
+        pltpu.VMEM((64, FT), f32),
+        pltpu.VMEM((64, d), bf16),
         pltpu.VMEM((n, 128, 128), bf16),
         pltpu.VMEM((n, 128, 128), bf16),
-        pltpu.VMEM((n, 8, 128), f32),
+        pltpu.VMEM((n, 1, 128), f32),
         pltpu.VMEM((2 * FT, d // 2), bf16),
         pltpu.VMEM((64, 2 * FT), bf16),
         pltpu.VMEM((64, d // 2), bf16),
         pltpu.VMEM((chips, rows, cols), bf16),
         pltpu.VMEM((nz, rows, cols), bf16),
-        sems((20,)),
+        sems((22,)),
         sems((28,)),
     ]
     dmd, wg = pl.pallas_call(
@@ -745,7 +750,7 @@
             jax.ShapeDtypeStruct((64, d), bf16),
         ),
         in_specs=[pl.BlockSpec(memory_space=pltpu.SMEM)] + [hbm] * 19,
-        out_specs=(vm, vm),
+        out_specs=(hbm, hbm),
         scratch_shapes=scratch,
         compiler_params=pltpu.CompilerParams(
             collective_id=0, has_side_effects=True, vmem_limit_bytes=62 * 1024 * 1024

time: 81.1 us -> 80.1 us (0.988)
  Pallas kernels: 76.8 us -> 75.8 us
    pallas_call x1, Pallas kernels: 76.8 us -> 75.8 us  [per_device(): pl.pallas_call(functools.partial(kernel, n, nz, blk), out_shape=(jax.Shap...]
where the time goes in v6:
time: 80.1 us; the launch traced here: 80 us
  Pallas kernels  75.8 us (95%)
  other arithmetic  2.23 us (3%)
  between operations  1.3 us (2%)
    pallas_call x1, Pallas kernels, per_device(): pl.pallas_call(functools.partial(kernel, n, nz, blk), out_shape=(jax.Shap...  75.8 us
    convert_element_type x1, other arithmetic, per_device(): return (dmd, wg.astype(f32))  2.23 us

profile of v6, /device:TPU:1, one launch (start us, length us, event | category | flops | bytes accessed | tf_op | source)
XLA Modules:
  0.0 80.0 jit_solution(8186511399630168149)
XLA Ops:
  1.3 75.8 %dmd.1 = (f32[1,64,128]{2,1,0:T(8,128)}, bf16[64,5120]{1,0:T(8,128)(2,1)}) custom-call(s32[1]{0:T(128)S(6)} %copy.23.step_ref, bf16[1,64,128]{2,1,0:T(8,128)(2,1)} %noise_h.1, f32[2,128]{1,0:T(2,128)} %gain_rh.1, f32[2,128]{1,0:T(2,128)} %gain_fh.1, bf16[3,8,5120]{2,1,0:T(8,128)(2,1)} %bitcast.2, bf16[3,8,5120]{2,1,0:T(8,128)(2,1)} %bitcast.3, ...), custom_call_target="tpu_custom_call" | custom-call | tf_op jit(solution)/shard_map/dmd/pallas_call | solution.py:746
  77.1 0.0 copy-start
  77.1 2.2 %convert_element_type.3 = f32[64,5120]{1,0:T(8,128)} convert(bf16[64,5120]{1,0:T(8,128)(2,1)} %get-tuple-element.5) | non-fusion elementwise | flops 327680 | bytes 1966080 | tf_op jit(solution)/shard_map/convert_element_type | solution.py:766
  79.4 0.0 copy-done
  79.4 0.6 copy.24
Async XLA Ops:
  77.1 2.2 %copy-start = (f32[1,64,128]{2,1,0:T(8,128)S(1)}, f32[1,64,128]{2,1,0:T(8,128)}, u32[]{:S(2)}) copy-start(f32[1,64,128]{2,1,0:T(8,128)} %get-tuple-element.8) | copy-start | bytes 98308

commit v7 on v6

--- a/solution.py
+++ b/solution.py
@@ -265,7 +265,8 @@
     pieces = (6 * groups + 1) // 2
     mod_rs, mod_ag, xl, xf = Lane(), Lane(), Lane(), Lane()
     nrm_rs, nrm_ag, tl, gl = Lane(), Lane(), Lane(), Lane()
-    hl, dl, w_rs, w_z, w_ag, w_fw = Lane(), Lane(), Lane(), Lane(), Lane(), Lane()
+    hl, dl = Lane(), Lane()
+    w_rs, w_z, w_ag, w_fw = [[Lane(), Lane()] for _ in range(4)]
     gy = GS // 2
     half_d = d // 2
     slot = pl.ds(pl.multiple_of(core * FT, FT), FT)
@@ -629,14 +630,24 @@
     rows = wrecv.shape[1]
     cols = wrecv.shape[2]
 
-    def piece(j, c):
+    first_cols = (cols // 128 + 1) // 2 * 128
+    parts = [(0, first_cols), (first_cols, cols - first_cols)]
+    parts = [p for p in parts if p[1]]
+
+    def piece(j, c, k):
+        at, size = parts[k]
         return (
             pl.ds(pl.multiple_of(j // gy * rows, 16), rows),
-            pl.ds(pl.multiple_of(c * half_d + lax.rem(j, gy) * cols, 128), cols),
+            pl.ds(pl.multiple_of(c * half_d + lax.rem(j, gy) * cols + at, 128), size),
         )
 
-    w_rs.mates(lambda j: wsend.at[piece(j, 0)], wrecv.at[chip])
-    wrecv[chip] = wsend[piece(chip, 0)]
+    def inner(k):
+        return pl.ds(*parts[k])
+
+    some = pl.ds(0, chips - 1)
+    for k in range(len(parts)):
+        w_rs[k].mates(lambda j: wsend.at[piece(j, 0, k)], wrecv.at[chip, :, inner(k)])
+        wrecv[chip, :, inner(k)] = wsend[piece(chip, 0, k)]
     ph("gap_wait")
     gl.wait(gapbuf.at[pl.ds(0, n - 1)])
     gap_all = jnp.sum(jnp.sum(gapbuf[...], axis=0), keepdims=True)
@@ -644,35 +655,70 @@
     dmd_ref[...] = dmd_ref[...] * inv
     put_dmd = load(dmd_ref, dmd_h.at[0])
     ph("w_wait")
-    w_rs.wait(wrecv.at[pl.ds(0, chips - 1)])
-    wsum = wrecv[0].astype(f32)
-    for j in range(1, chips):
-        wsum = wsum + wrecv[j].astype(f32)
-    zbuf[mz] = (wsum * (inv / math.sqrt(nz * tokens))).astype(bf16)
+    scale = inv / math.sqrt(nz * tokens)
+    for k in range(len(parts)):
+        w_rs[k].wait(wrecv.at[some, :, inner(k)])
+        wsum = wrecv[0, :, inner(k)].astype(f32)
+        for j in range(1, chips):
+            wsum = wsum + wrecv[j, :, inner(k)].astype(f32)
+        zbuf[mz, :, inner(k)] = (wsum * scale).astype(bf16)
+        mine_z = zbuf.at[mz, :, inner(k)]
+        for i in range(1, nz):
+            w_z[k].to(mine_z, mine_z, lax.rem(mz + i, nz), "batch").start()
     ph("w_z")
-    for i in range(1, nz):
-        w_z.to(zbuf.at[mz], zbuf.at[mz], lax.rem(mz + i, nz), "batch").start()
-    if nz > 1:
-        zview = zbuf.at[pl.ds(0, nz - 1)]
-        zwait = w_z.to(zview, zview, lax.rem(mz + 1, nz), "batch")
-        zwait.wait_recv()
-        zwait.wait_send()
-    whole = zbuf[0].astype(f32)
-    for z in range(1, nz):
-        whole = whole + zbuf[z].astype(f32)
+    for k in range(len(parts)):
+        if nz > 1:
+            zview = zbuf.at[pl.ds(0, nz - 1), :, inner(k)]
+            zwait = w_z[k].to(zview, zview, lax.rem(mz + 1, nz), "batch")
+            zwait.wait_recv()
+            zwait.wait_send()
+        whole = zbuf[0, :, inner(k)].astype(f32)
+        for z in range(1, nz):
+            whole = whole + zbuf[z, :, inner(k)].astype(f32)
+        part = wg_ref.at[piece(chip, core, k)]
+        part[...] = whole.astype(bf16)
+        w_ag[k].mates(lambda j: part, part)
     ph("w_ag")
-    part = wg_ref.at[piece(chip, core)]
-    part[...] = whole.astype(bf16)
-    w_ag.mates(lambda j: part, part)
-    w_ag.wait(wrecv.at[pl.ds(0, chips - 1)])
+    for k in range(len(parts)):
+        at, size = parts[k]
+        w_ag[k].wait(wrecv.at[some, :, inner(k)])
+        for y in range(gy):
+            col = pl.ds(pl.multiple_of(core * half_d + y * cols + at, 128), size)
+            w_fw[k].to(wg_ref.at[:, col], wg_h.at[:, col], other).start()
     ph("w_forward")
-    w_fw.to(wg_ref.at[:, half_of(core)], wg_h.at[:, half_of(core)], other).start()
     put_wg = load(wg_ref.at[:, half_of(core)], wg_h.at[:, half_of(core)])
     put_dmd.wait()
     put_wg.wait()
-    w_fw.to(wg_ref.at[:, half_of(core)], wg_h.at[:, half_of(1 - core)], other).wait_recv()
-    w_fw.to(wg_ref.at[:, half_of(core)], wg_h.at[:, half_of(core)], other).wait_send()
+    for k in range(len(parts)):
+        view = pl.ds(0, gy * parts[k][1])
+        fwait = w_fw[k].to(wg_ref.at[:, view], wg_h.at[:, view], other)
+        fwait.wait_recv()
+        fwait.wait_send()
     ph(None)
+
+
+def widen(a_h, b_h, a_out, b_out, a_v, b_v, c_v, sem):
+    step = 1024
+    parts = b_v.shape[1] // step
+    ins = []
+    outs = []
+    for k in range(parts):
+        cols = pl.ds(k * step, step)
+        ins.append(pltpu.make_async_copy(b_h.at[:, cols], b_v.at[:, cols], sem.at[k]))
+        outs.append(pltpu.make_async_copy(c_v.at[:, cols], b_out.at[:, cols], sem.at[parts + k]))
+        ins[k].start()
+    a_in = pltpu.make_async_copy(a_h, a_v, sem.at[2 * parts])
+    a_go = pltpu.make_async_copy(a_v, a_out, sem.at[2 * parts + 1])
+    a_in.start()
+    for k in range(parts):
+        cols = pl.ds(k * step, step)
+        ins[k].wait()
+        c_v[:, cols] = b_v[:, cols].astype(f32)
+        outs[k].start()
+    a_in.wait()
+    a_go.start()
+    for c in outs + [a_go]:
+        c.wait()
 
 
 def per_device(
@@ -741,7 +787,7 @@
         pltpu.VMEM((chips, rows, cols), bf16),
         pltpu.VMEM((nz, rows, cols), bf16),
         sems((22,)),
-        sems((28,)),
+        sems((36,)),
     ]
     dmd, wg = pl.pallas_call(
         functools.partial(kernel, n, nz, blk),
@@ -763,7 +809,23 @@
         out_real, out_fake,
         query_real, key_real, value_real, query_fake, key_fake, value_fake,
     )
-    return dmd, wg.astype(f32)
+    return pl.pallas_call(
+        widen,
+        out_shape=(
+            jax.ShapeDtypeStruct((1, 64, FT), f32),
+            jax.ShapeDtypeStruct((64, d), f32),
+        ),
+        in_specs=[hbm, hbm],
+        out_specs=(hbm, hbm),
+        scratch_shapes=[
+            pltpu.VMEM((1, 64, FT), f32),
+            pltpu.VMEM((64, d), bf16),
+            pltpu.VMEM((64, d), f32),
+            sems((2 * (d // 1024) + 2,)),
+        ],
+        compiler_params=pltpu.CompilerParams(vmem_limit_bytes=62 * 1024 * 1024),
+        name="widen",
+    )(dmd, wg)
 
 
 def solution(mesh):

time: 80.1 us -> 79.1 us (0.988)
  other arithmetic: 2.23 us -> 0 us
  Pallas kernels: 75.8 us -> 77.5 us
    convert_element_type x1 -> x0, other arithmetic: 2.23 us -> none  [per_device(): return (dmd, wg.astype(f32))]
    pallas_call x0 -> x1, Pallas kernels: none -> 2.08 us  [per_device(): pl.pallas_call(widen, out_shape=(jax.ShapeDtypeStruct((1, 64, FT), f32),...]
where the time goes in v7:
time: 79.1 us; the launch traced here: 79 us
  Pallas kernels  77.5 us (98%)
  between operations  1.45 us (2%)
    pallas_call x1, Pallas kernels, per_device(): pl.pallas_call(functools.partial(kernel, n, nz, blk), out_shape=(jax.Shap...  75.5 us
    pallas_call x1, Pallas kernels, per_device(): pl.pallas_call(widen, out_shape=(jax.ShapeDtypeStruct((1, 64, FT), f32),...  2.08 us

profile of v7, /device:TPU:1, one launch (start us, length us, event | category | flops | bytes accessed | tf_op | source)
XLA Modules:
  0.0 79.0 jit_solution(18178997423100526182)
XLA Ops:
  1.3 75.5 %dmd.1 = (f32[1,64,128]{2,1,0:T(8,128)}, bf16[64,5120]{1,0:T(8,128)(2,1)}) custom-call(s32[1]{0:T(128)S(6)} %copy.22.step_ref, bf16[1,64,128]{2,1,0:T(8,128)(2,1)} %noise_h.1, f32[2,128]{1,0:T(2,128)} %gain_rh.1, f32[2,128]{1,0:T(2,128)} %gain_fh.1, bf16[3,8,5120]{2,1,0:T(8,128)(2,1)} %bitcast.2, bf16[3,8,5120]{2,1,0:T(8,128)(2,1)} %bitcast.3, ...), custom_call_target="tpu_custom_call" | custom-call | tf_op jit(solution)/shard_map/dmd/pallas_call | solution.py:792
  76.7 2.1 %widen.1 = (f32[1,64,128]{2,1,0:T(8,128)}, f32[64,5120]{1,0:T(8,128)}) custom-call(f32[1,64,128]{2,1,0:T(8,128)} %get-tuple-element.4.a_h, bf16[64,5120]{1,0:T(8,128)(2,1)} %get-tuple-element.5.b_h), custom_call_target="tpu_custom_call" | custom-call | tf_op jit(solution)/shard_map/widen/pallas_call | solution.py:812
